TPU v7x, 32 devices: a whole 2x2x4 slice. The times are simulated.
32 devices in a mesh: frame: 4 (over x, core), fsdp: 4 (over z), head: 2 (over y).
Axes of the slice: x: 2, y: 2, z: 4, core: 2. Of those that a mesh axis runs over, the one named last changes fastest.
Arguments:
- queries: bfloat16 [1024, 10240], P('frame', ('fsdp', 'head')), may hold values from -6 to 6
- noisy_keys: bfloat16 [1024, 10240], P('frame', ('fsdp', 'head')), may hold values from -6 to 6
- noisy_values: bfloat16 [1024, 10240], P('frame', ('fsdp', 'head')), may hold values from -6 to 6
- clean_keys: bfloat16 [1024, 10240], P('frame', ('fsdp', 'head')), may hold values from -10 to 10
- clean_values: bfloat16 [1024, 10240], P('frame', ('fsdp', 'head')), may hold values from -6 to 6
- gain_query: float32 [5120], replicated, may hold values from 0.5 to 2
- gain_key: float32 [5120], replicated, may hold values from 0.5 to 2
- out_grad: bfloat16 [1024, 10240], P('frame', ('fsdp', 'head')), may hold values from -6 to 6
Outputs:
- attended: bfloat16 [1024, 10240], P('frame', ('fsdp', 'head'))
- grad_queries: bfloat16 [1024, 10240], P('frame', ('fsdp', 'head'))
- grad_keys: bfloat16 [1024, 10240], P('frame', ('fsdp', 'head'))
- grad_values: bfloat16 [1024, 10240], P('frame', ('fsdp', 'head'))
- grad_gain_query: float32 [5120], replicated
- grad_gain_key: float32 [5120], replicated
All inputs are finite; a program needn't handle non-finite values.
Results may differ from a plain program's by a relative error of at most 0.012.
Values may be sent and summed in bfloat16 or wider, within the bound.
A program may use at most 64 MiB of HBM per device.

v0:
```python
import functools
import math

import jax
import jax.numpy as jnp
from jax import lax
from jax.experimental import pallas as pl
from jax.experimental.pallas import tpu as pltpu
from jax.sharding import PartitionSpec as P

DH = 128
EPSILON = 1e-06
MESH = pl.DeviceIdType.MESH
VMEM_BYTES = 67043328
F32 = jnp.float32
BF16 = jnp.bfloat16


def dot_nt(a, b):
    return lax.dot_general(a, b, (((1,), (1,)), ((), ())), preferred_element_type=F32)


def dot_nn(a, b):
    return lax.dot_general(a, b, (((1,), (0,)), ((), ())), preferred_element_type=F32)


def dot_tn(a, b):
    return lax.dot_general(a, b, (((0,), (0,)), ((), ())), preferred_element_type=F32)


def kernel(
    frames, fsdp, heads_axis, width, features,
    q_hbm, k_hbm, v_hbm, ck_hbm, cv_hbm, gq_hbm, gk_hbm, g_hbm,
    att_out, dq_out, dk_out, dv_out, gain_q_out, gain_k_out,
    q, k, v, g, gq, gk, cks, cvs, flat_q, flat_k, inner_q, inner_k, rates,
    stats, sums1, sums2,
    load_sem, own_send, relay_send, clean_recv, stats_send, stats_recv, s1_send, s1_recv, s2_send, s2_recv,
):
    length = q.shape[0]
    head_count = width // DH
    videos = fsdp // 2
    scaling = 1.0 / math.sqrt(DH)
    power = scaling * math.log2(math.e)
    frame = lax.axis_index("frame")
    fs = lax.axis_index("fsdp")
    half = fs // videos
    video = lax.rem(fs, videos)
    me1 = frame * videos + video
    n1 = frames * videos
    me2 = half * heads_axis + lax.axis_index("head")
    n2 = 2 * heads_axis

    def peer1(distance):
        p = lax.rem(me1 + distance, n1)
        return {"frame": p // videos, "fsdp": half * videos + lax.rem(p, videos)}

    def peer2(distance):
        p = lax.rem(me2 + distance, n2)
        return {"fsdp": (p // heads_axis) * videos + video, "head": lax.rem(p, heads_axis)}

    barrier = pltpu.get_barrier_semaphore()

    def greet(d, _):
        pl.semaphore_signal(barrier, inc=1, device_id=peer1(d), device_id_type=MESH)
        return 0

    lax.fori_loop(1, n1, greet, 0)
    for d in range(1, n2):
        pl.semaphore_signal(barrier, inc=1, device_id=peer2(d), device_id_type=MESH)
    start = pl.multiple_of(me2 * width, DH)
    loads = []
    for i, (src, dst) in enumerate(
        (
            (q_hbm, q),
            (k_hbm, k),
            (gq_hbm.at[:, pl.ds(start, width)], gq),
            (gk_hbm.at[:, pl.ds(start, width)], gk),
            (v_hbm, v),
            (g_hbm, g),
        )
    ):
        copy = pltpu.make_async_copy(src, dst, load_sem.at[i])
        copy.start()
        loads.append(copy)
    pl.semaphore_wait(barrier, n1 - 1 + n2 - 1)

    def columns(h):
        return pl.ds(pl.multiple_of(h * DH, DH), DH)

    def clean_copy(j, h, kv, target, sends, own):
        cols = columns(h)
        land = (cks, cvs)[kv].at[j, :, cols]
        src = (ck_hbm, cv_hbm)[kv].at[:, cols] if own else land
        return pltpu.make_async_remote_copy(
            src_ref=src,
            dst_ref=land,
            send_sem=sends.at[h, kv],
            recv_sem=clean_recv.at[j, h, kv],
            device_id={"frame": jnp.int32(target)},
            device_id_type=MESH,
        )

    def plan(nb):
        pair, side = nb // 2, nb % 2
        partner, further = 2 * pair + 1 - side, nb + 2
        direct = [2 * c + side for c in range(pair)]
        relayed = [2 * c + 1 - side for c in range(pair)] + ([nb - 1] if side else [])
        own = ([further] if further < frames else []) + ([partner] if side == 0 else [])
        passes = [partner] + ([further] if further < frames else [])
        return direct, relayed, own, passes

    for nb in range(frames):
        _, _, own, _ = plan(nb)
        if own:

            @pl.when(frame == nb)
            def _():
                def go(h, _):
                    for t, target in enumerate(own):
                        for kv in range(2):
                            clean_copy(nb, h, kv, target, own_send.at[t], True).start()
                    return 0

                lax.fori_loop(0, head_count, go, 0)

    row = lax.broadcasted_iota(jnp.int32, (8, length), 0)

    def as_rows(a, b):
        a = jnp.sum(jnp.transpose(a), axis=0, keepdims=True)
        b = jnp.sum(jnp.transpose(b), axis=0, keepdims=True)
        return jnp.where(row == 0, a, jnp.where(row == 1, b, 0.0))

    def stats_copy(phase, d, slot):
        return pltpu.make_async_remote_copy(
            src_ref=stats.at[phase, slot],
            dst_ref=stats.at[phase, slot],
            send_sem=stats_send.at[phase, d],
            recv_sem=stats_recv.at[phase, d],
            device_id=peer2(d),
            device_id_type=MESH,
        )

    def stats_go(phase, value):
        stats[phase, me2] = value
        for d in range(1, n2):
            stats_copy(phase, d, me2).start()

    def stats_total(phase):
        for d in range(1, n2):
            stats_copy(phase, d, lax.rem(me2 + n2 - d, n2)).wait_recv()
        return jnp.sum(stats[phase], axis=0)

    loads[0].wait()
    loads[1].wait()

    def square(ref):
        total = jnp.zeros((length, DH), F32)
        for h in range(head_count):
            x = ref[:, h * DH : (h + 1) * DH].astype(F32)
            total = total + x * x
        return total

    stats_go(0, as_rows(square(q), square(k)))
    inner_q[...] = jnp.zeros_like(inner_q)
    inner_k[...] = jnp.zeros_like(inner_k)
    for copy in loads[2:]:
        copy.wait()
    rates[...] = jnp.transpose(lax.rsqrt(stats_total(0) / features + EPSILON))

    def head_step(nb, h):
        direct, relayed, _, passes = plan(nb)
        cols = columns(h)
        for j in direct:
            for kv in range(2):
                clean_copy(j, h, kv, passes[0], relay_send.at[0, j], False).wait_recv()
                for t, target in enumerate(passes):
                    clean_copy(j, h, kv, target, relay_send.at[t, j], False).start()
        rate_q = rates[:, 0:1]
        rate_k = rates[:, 1:2]
        q_full = q[:, cols].astype(F32)
        k_full = k[:, cols].astype(F32)
        gain_q = gq[:, cols]
        gain_k = gk[:, cols]
        qn = (q_full * rate_q * gain_q).astype(BF16)
        kn = (k_full * rate_k * gain_k).astype(BF16)
        val = v[:, cols]
        grad = g[:, cols]
        scores = [dot_nt(qn, kn)]
        grad_probs = [dot_nt(grad, val)]
        for j in relayed:
            for kv in range(2):
                clean_copy(j, h, kv, passes[0], relay_send.at[0, j], False).wait_recv()
        for j in range(nb):
            scores.append(dot_nt(qn, cks[j, :, cols]))
            grad_probs.append(dot_nt(grad, cvs[j, :, cols]))
        top = functools.reduce(jnp.maximum, [jnp.max(s, axis=1, keepdims=True) for s in scores])
        expo = [jnp.exp2((s - top) * power) for s in scores]
        total = functools.reduce(jnp.add, [jnp.sum(e, axis=1, keepdims=True) for e in expo])
        summed = dot_nn(expo[0].astype(BF16), val)
        for j in range(nb):
            summed = summed + dot_nn(expo[j + 1].astype(BF16), cvs[j, :, cols])
        inverse = 1.0 / total
        attention = summed * inverse
        att_out[:, cols] = attention.astype(BF16)
        delta = jnp.sum(grad.astype(F32) * attention, axis=1, keepdims=True)
        probs = [e * inverse for e in expo]
        grad_scores = [(p * (d - delta)).astype(BF16) for p, d in zip(probs, grad_probs)]
        grad_qn = dot_nn(grad_scores[0], kn)
        for j in range(nb):
            grad_qn = grad_qn + dot_nn(grad_scores[j + 1], cks[j, :, cols])
        grad_qn = grad_qn * scaling
        grad_kn = dot_tn(grad_scores[0], qn) * scaling
        dv_out[:, cols] = dot_tn(probs[0].astype(BF16), grad).astype(BF16)
        fq = grad_qn * gain_q
        fk = grad_kn * gain_k
        flat_q[:, cols] = fq
        flat_k[:, cols] = fk
        inner_q[...] += q_full * fq
        inner_k[...] += k_full * fk
        sums1[me1, 0:1, cols] = jnp.sum(grad_qn * q_full * rate_q, axis=0, keepdims=True)
        sums1[me1, 1:2, cols] = jnp.sum(grad_kn * k_full * rate_k, axis=0, keepdims=True)

    for nb in range(frames):

        @pl.when(frame == nb)
        def _():
            def step(h, _):
                head_step(nb, h)
                return 0

            lax.fori_loop(0, head_count, step, 0)

    stats_go(1, as_rows(inner_q[...], inner_k[...]))

    def s1_copy(d, slot):
        return pltpu.make_async_remote_copy(
            src_ref=sums1.at[slot],
            dst_ref=sums1.at[slot],
            send_sem=s1_send.at[d],
            recv_sem=s1_recv.at[d],
            device_id=peer1(d),
            device_id_type=MESH,
        )

    def s2_copy(d, slot):
        return pltpu.make_async_remote_copy(
            src_ref=sums2.at[slot],
            dst_ref=sums2.at[slot],
            send_sem=s2_send.at[d],
            recv_sem=s2_recv.at[d],
            device_id=peer2(d),
            device_id_type=MESH,
        )

    def s1_go(d, _):
        s1_copy(d, me1).start()
        return 0

    lax.fori_loop(1, n1, s1_go, 0)

    inners = jnp.transpose(stats_total(1))
    rate_q = rates[:, 0:1]
    rate_k = rates[:, 1:2]
    cube_q = rate_q * rate_q * rate_q * inners[:, 0:1] / features
    cube_k = rate_k * rate_k * rate_k * inners[:, 1:2] / features

    def s1_land(d, _):
        s1_copy(d, lax.rem(me1 + n1 - d, n1)).wait_recv()
        return 0

    lax.fori_loop(1, n1, s1_land, 0)
    sums2[me2] = jnp.sum(sums1[...], axis=0)
    for d in range(1, n2):
        s2_copy(d, me2).start()

    def finish(h, _):
        cols = columns(h)
        dq_out[:, cols] = (rate_q * flat_q[:, cols] - q[:, cols].astype(F32) * cube_q).astype(BF16)
        dk_out[:, cols] = (rate_k * flat_k[:, cols] - k[:, cols].astype(F32) * cube_k).astype(BF16)
        return 0

    lax.fori_loop(0, head_count, finish, 0)
    for d in range(1, n2):
        s2_copy(d, lax.rem(me2 + n2 - d, n2)).wait_recv()
    for p in range(n2):
        gain_q_out[:, p * width : (p + 1) * width] = sums2[p, 0:1, :]
        gain_k_out[:, p * width : (p + 1) * width] = sums2[p, 1:2, :]

    for d in range(1, n2):
        stats_copy(0, d, me2).wait_send()
        stats_copy(1, d, me2).wait_send()
        s2_copy(d, me2).wait_send()

    def s1_gone(d, _):
        s1_copy(d, me1).wait_send()
        return 0

    lax.fori_loop(1, n1, s1_gone, 0)
    for nb in range(frames):
        direct, _, own, passes = plan(nb)

        @pl.when(frame == nb)
        def _():
            def gone(h, _):
                for kv in range(2):
                    for t, target in enumerate(own):
                        clean_copy(nb, h, kv, target, own_send.at[t], True).wait_send()
                    for j in direct:
                        for t, target in enumerate(passes):
                            clean_copy(j, h, kv, target, relay_send.at[t, j], False).wait_send()
                return 0

            lax.fori_loop(0, head_count, gone, 0)


def write_out(*refs):
    sem = refs[12]
    copies = [pltpu.make_async_copy(refs[i], refs[6 + i], sem.at[i]) for i in range(6)]
    for copy in copies:
        copy.start()
    for copy in copies:
        copy.wait()


def on_device(queries, noisy_keys, noisy_values, clean_keys, clean_values, gain_query, gain_key, out_grad):
    length, width = queries.shape
    features = gain_query.shape[0]
    frames = lax.axis_size("frame")
    fsdp = lax.axis_size("fsdp")
    heads_axis = lax.axis_size("head")
    head_count = width // DH
    n1 = frames * (fsdp // 2)
    n2 = 2 * heads_axis
    block = pltpu.VMEM((length, width), BF16)
    gains = pltpu.VMEM((1, features), F32)
    anywhere = pl.BlockSpec(memory_space=pl.ANY)
    vmem = pl.BlockSpec(memory_space=pltpu.VMEM)
    dma = pltpu.SemaphoreType.DMA
    earlier = max(frames - 1, 1)
    kept = 4 * 2 * length * width + 2 * 4 * features
    outs = pl.pallas_call(
        functools.partial(kernel, frames, fsdp, heads_axis, width, features),
        out_shape=(block, block, block, block, gains, gains),
        in_specs=[anywhere] * 8,
        out_specs=[vmem] * 6,
        scratch_shapes=[
            pltpu.VMEM((length, width), BF16),
            pltpu.VMEM((length, width), BF16),
            pltpu.VMEM((length, width), BF16),
            pltpu.VMEM((length, width), BF16),
            pltpu.VMEM((1, width), F32),
            pltpu.VMEM((1, width), F32),
            pltpu.VMEM((earlier, length, width), BF16),
            pltpu.VMEM((earlier, length, width), BF16),
            pltpu.VMEM((length, width), F32),
            pltpu.VMEM((length, width), F32),
            pltpu.VMEM((length, DH), F32),
            pltpu.VMEM((length, DH), F32),
            pltpu.VMEM((length, 8), F32),
            pltpu.VMEM((2, n2, 8, length), F32),
            pltpu.VMEM((n1, 2, width), F32),
            pltpu.VMEM((n2, 2, width), F32),
            dma((6,)),
            dma((2, head_count, 2)),
            dma((2, earlier, head_count, 2)),
            dma((earlier, head_count, 2)),
            dma((2, n2)),
            dma((2, n2)),
            dma((n1,)),
            dma((n1,)),
            dma((n2,)),
            dma((n2,)),
        ],
        compiler_params=pltpu.CompilerParams(
            collective_id=0, has_side_effects=True, vmem_limit_bytes=VMEM_BYTES - kept - 4096
        ),
        name="attention",
    )(
        queries, noisy_keys, noisy_values, clean_keys, clean_values,
        gain_query.reshape(1, features), gain_key.reshape(1, features), out_grad,
    )
    outs = pl.pallas_call(
        write_out,
        out_shape=tuple(jax.ShapeDtypeStruct(out.shape, out.dtype) for out in outs),
        in_specs=[anywhere] * 6,
        out_specs=[anywhere] * 6,
        scratch_shapes=[dma((6,))],
        compiler_params=pltpu.CompilerParams(vmem_limit_bytes=8 * 1024 * 1024),
        name="write_out",
    )(*outs)
    return (*outs[:4], outs[4].reshape(features), outs[5].reshape(features))


def solution(mesh):
    tokens = P("frame", ("fsdp", "head"))
    return jax.shard_map(
        on_device,
        mesh=mesh,
        in_specs=(tokens, tokens, tokens, tokens, tokens, P(), P(), tokens),
        out_specs=(tokens, tokens, tokens, tokens, P(), P()),
        check_vma=False,
    )
```

profile of v0, /device:TPU:0, one launch (start us, length us, event | category | flops | bytes accessed | tf_op | source)
XLA Modules:
  0.0 50.3 jit_solution(5487505753093458035)
XLA Ops:
  0.6 48.1 %attention.1 = (bf16[256,1280]{1,0:T(8,128)(2,1)S(1)}, bf16[256,1280]{1,0:T(8,128)(2,1)S(1)}, bf16[256,1280]{1,0:T(8,128)(2,1)S(1)}, bf16[256,1280]{1,0:T(8,128)...) custom-call(bf16[256,1280]{1,0:T(8,128)(2,1)} %q_hbm.1, bf16[256,1280]{1,0:T(8,128)(2,1)} %k_hbm.1, ...), custom_call_target="tpu_custom_call" | custom-call | tf_op jit(solution)/shard_map/attention/pallas_call | solution.py:341
  48.8 1.5 %write_out.1 = (bf16[256,1280]{1,0:T(8,128)(2,1)}, bf16[256,1280]{1,0:T(8,128)(2,1)}, bf16[256,1280]{1,0:T(8,128)(2,1)}, bf16[256,1280]{1,0:T(8,128)(2,1)}, f32[1,5120]{1,0:T(1,128)}, /*index=5*/f32[1,5120]{1,0:T(1,128)}) custom-call(bf16[256,1280]{1,0:T(8,128)(2,1)S(1)} %get-tuple-element.18.refs_0_, bf16[256,1280]{1,0:T(8,128)(2,1)S(1)} %get-tuple-element.19.refs_1_, ...), custom_call_target="tpu_custom_call" | custom-call | tf_op jit(solution)/shard_map/write_out/pallas_call | solution.py:382
where the time goes:
time: 50.5 us; the launch traced here: 50.3 us
  Pallas kernels  49.7 us (98%)
  between operations  0.64 us (1%)
    pallas_call x1, Pallas kernels, on_device(): pl.pallas_call(functools.partial(kernel, frames, fsdp, heads_axis, width,...  48.1 us
    pallas_call x1, Pallas kernels, on_device(): pl.pallas_call(write_out, out_shape=tuple((jax.ShapeDtypeStruct(out.shape...  1.54 us

commit v1 on v0

--- a/solution.py
+++ b/solution.py
@@ -29,15 +29,18 @@
 
 
 def kernel(
-    frames, fsdp, heads_axis, width, features,
+    frames, fsdp, heads_axis, width, features, lent,
     q_hbm, k_hbm, v_hbm, ck_hbm, cv_hbm, gq_hbm, gk_hbm, g_hbm,
     att_out, dq_out, dk_out, dv_out, gain_q_out, gain_k_out,
     q, k, v, g, gq, gk, cks, cvs, flat_q, flat_k, inner_q, inner_k, rates,
-    stats, sums1, sums2,
+    stats, sums1, sums2, far_q, far_g, far_rates, far_inner, part, back_out, back_in,
+    near_trip, far_trip, trip_out, trip_in, row_out, row_in,
     load_sem, own_send, relay_send, clean_recv, stats_send, stats_recv, s1_send, s1_recv, s2_send, s2_recv,
+    stage_sem, far_send, far_recv, back_send, back_recv, trip_send, trip_recv, row_send, row_recv,
 ):
     length = q.shape[0]
     head_count = width // DH
+    kept = head_count - lent
     videos = fsdp // 2
     scaling = 1.0 / math.sqrt(DH)
     power = scaling * math.log2(math.e)
@@ -57,6 +60,32 @@
     def peer2(distance):
         p = lax.rem(me2 + distance, n2)
         return {"fsdp": (p // heads_axis) * videos + video, "head": lax.rem(p, heads_axis)}
+
+    def columns(h):
+        return pl.ds(pl.multiple_of(h * DH, DH), DH)
+
+    def repeat(first, last, step):
+        def body(i, _):
+            step(i)
+            return 0
+
+        lax.fori_loop(first, last, body, 0)
+
+    def stage_copy(nb, h, kv):
+        cols = columns(h)
+        return pltpu.make_async_copy(
+            (ck_hbm, cv_hbm)[kv].at[:, cols], (cks, cvs)[kv].at[nb, :, cols], stage_sem.at[h, kv]
+        )
+
+    for nb in range(frames - 1):
+
+        @pl.when(frame == nb)
+        def _():
+            def stage(h):
+                for kv in range(2):
+                    stage_copy(nb, h, kv).start()
+
+            repeat(0, head_count, stage)
 
     barrier = pltpu.get_barrier_semaphore()
 
@@ -84,44 +113,93 @@
         loads.append(copy)
     pl.semaphore_wait(barrier, n1 - 1 + n2 - 1)
 
-    def columns(h):
-        return pl.ds(pl.multiple_of(h * DH, DH), DH)
-
-    def clean_copy(j, h, kv, target, sends, own):
-        cols = columns(h)
-        land = (cks, cvs)[kv].at[j, :, cols]
-        src = (ck_hbm, cv_hbm)[kv].at[:, cols] if own else land
+    def frame_copy(src, dst, send, recv, target):
         return pltpu.make_async_remote_copy(
             src_ref=src,
-            dst_ref=land,
-            send_sem=sends.at[h, kv],
-            recv_sem=clean_recv.at[j, h, kv],
+            dst_ref=dst,
+            send_sem=send,
+            recv_sem=recv,
             device_id={"frame": jnp.int32(target)},
             device_id_type=MESH,
         )
+
+    def clean_copy(j, h, kv, target, sends):
+        land = (cks, cvs)[kv].at[j, :, columns(h)]
+        return frame_copy(land, land, sends.at[h, kv], clean_recv.at[j, h, kv], target)
 
     def plan(nb):
         pair, side = nb // 2, nb % 2
         partner, further = 2 * pair + 1 - side, nb + 2
         direct = [2 * c + side for c in range(pair)]
         relayed = [2 * c + 1 - side for c in range(pair)] + ([nb - 1] if side else [])
-        own = ([further] if further < frames else []) + ([partner] if side == 0 else [])
+        own = ([(0, further)] if further < frames else []) + ([(1, partner)] if side == 0 else [])
         passes = [partner] + ([further] if further < frames else [])
         return direct, relayed, own, passes
 
+    def helps(nb):
+        return lent > 0 and nb < 2
+
+    def helped(nb):
+        return lent > 0 and nb >= 2
+
+    def own_lists(nb):
+        own = plan(nb)[2]
+        if not helps(nb):
+            return own, own, own
+        return own, [o for o in own if o[0] == 1], [(1, 1 - nb)]
+
+    def send_own(nb, h, targets):
+        for kv in range(2):
+            for t, target in targets:
+                clean_copy(nb, h, kv, target, own_send.at[t]).start()
+
+    def far_copy(kind, r, target):
+        if kind == 0:
+            src, land = q_hbm, far_q
+        else:
+            src, land = g_hbm, far_g
+        return frame_copy(
+            src.at[:, columns(kept + r)], land.at[r], far_send.at[kind, r], far_recv.at[kind, r], target
+        )
+
+    def back_copy(kind, r, target):
+        return frame_copy(
+            back_out.at[kind, r], back_in.at[kind, r], back_send.at[kind, r], back_recv.at[kind, r], target
+        )
+
+    def trip_copy(target):
+        return frame_copy(trip_out, trip_in, trip_send.at[0], trip_recv.at[0], target)
+
+    def row_copy(target):
+        return frame_copy(row_out, row_in, row_send.at[0], row_recv.at[0], target)
+
+    def lend(nb, first, last):
+        def go(r):
+            for kind in range(2):
+                far_copy(kind, r, nb - 2).start()
+
+        repeat(first, last, go)
+
     for nb in range(frames):
-        _, _, own, _ = plan(nb)
-        if own:
-
-            @pl.when(frame == nb)
-            def _():
-                def go(h, _):
-                    for t, target in enumerate(own):
+        full, late, lends = own_lists(nb)
+
+        @pl.when(frame == nb)
+        def _():
+            if helped(nb):
+                lend(nb, 0, lent // 2)
+            if nb < frames - 1:
+
+                def go(targets):
+                    def step(h):
                         for kv in range(2):
-                            clean_copy(nb, h, kv, target, own_send.at[t], True).start()
-                    return 0
-
-                lax.fori_loop(0, head_count, go, 0)
+                            stage_copy(nb, h, kv).wait()
+                        send_own(nb, h, targets)
+
+                    return step
+
+                repeat(0, kept - 1, go(full))
+                repeat(kept - 1, kept, go(late))
+                repeat(kept, head_count, go(lends))
 
     row = lax.broadcasted_iota(jnp.int32, (8, length), 0)
 
@@ -165,16 +243,35 @@
     inner_k[...] = jnp.zeros_like(inner_k)
     for copy in loads[2:]:
         copy.wait()
-    rates[...] = jnp.transpose(lax.rsqrt(stats_total(0) / features + EPSILON))
+    rate_rows = lax.rsqrt(stats_total(0) / features + EPSILON)
+    rates[...] = jnp.transpose(rate_rows)
+    for nb in range(frames):
+        if helped(nb):
+
+            @pl.when(frame == nb)
+            def _():
+                row_out[...] = rate_rows
+                row_copy(nb - 2).start()
+                lend(nb, lent // 2, lent)
+
+    def store_grads(cols, q_full, k_full, grad_qn, grad_kn):
+        fq = grad_qn * gq[:, cols]
+        fk = grad_kn * gk[:, cols]
+        flat_q[:, cols] = fq
+        flat_k[:, cols] = fk
+        inner_q[...] += q_full * fq
+        inner_k[...] += k_full * fk
+        sums1[me1, 0:1, cols] = jnp.sum(grad_qn * q_full * rates[:, 0:1], axis=0, keepdims=True)
+        sums1[me1, 1:2, cols] = jnp.sum(grad_kn * k_full * rates[:, 1:2], axis=0, keepdims=True)
 
     def head_step(nb, h):
         direct, relayed, _, passes = plan(nb)
         cols = columns(h)
         for j in direct:
             for kv in range(2):
-                clean_copy(j, h, kv, passes[0], relay_send.at[0, j], False).wait_recv()
+                clean_copy(j, h, kv, passes[0], relay_send.at[0, j]).wait_recv()
                 for t, target in enumerate(passes):
-                    clean_copy(j, h, kv, target, relay_send.at[t, j], False).start()
+                    clean_copy(j, h, kv, target, relay_send.at[t, j]).start()
         rate_q = rates[:, 0:1]
         rate_k = rates[:, 1:2]
         q_full = q[:, cols].astype(F32)
@@ -189,7 +286,7 @@
         grad_probs = [dot_nt(grad, val)]
         for j in relayed:
             for kv in range(2):
-                clean_copy(j, h, kv, passes[0], relay_send.at[0, j], False).wait_recv()
+                clean_copy(j, h, kv, passes[0], relay_send.at[0, j]).wait_recv()
         for j in range(nb):
             scores.append(dot_nt(qn, cks[j, :, cols]))
             grad_probs.append(dot_nt(grad, cvs[j, :, cols]))
@@ -211,26 +308,133 @@
         grad_qn = grad_qn * scaling
         grad_kn = dot_tn(grad_scores[0], qn) * scaling
         dv_out[:, cols] = dot_tn(probs[0].astype(BF16), grad).astype(BF16)
-        fq = grad_qn * gain_q
-        fk = grad_kn * gain_k
-        flat_q[:, cols] = fq
-        flat_k[:, cols] = fk
-        inner_q[...] += q_full * fq
-        inner_k[...] += k_full * fk
-        sums1[me1, 0:1, cols] = jnp.sum(grad_qn * q_full * rate_q, axis=0, keepdims=True)
-        sums1[me1, 1:2, cols] = jnp.sum(grad_kn * k_full * rate_k, axis=0, keepdims=True)
+        store_grads(cols, q_full, k_full, grad_qn, grad_kn)
+
+    def merged(mine, theirs):
+        top1, total1, dot1 = [mine[:, i : i + 1] for i in range(3)]
+        top2, total2, dot2 = [theirs[:, i : i + 1] for i in range(3)]
+        top = jnp.maximum(top1, top2)
+        weight1 = jnp.exp2((top1 - top) * power)
+        weight2 = jnp.exp2((top2 - top) * power)
+        inverse = 1.0 / (total1 * weight1 + total2 * weight2)
+        delta = (dot1 * weight1 + dot2 * weight2) * inverse
+        return top, inverse, delta, weight1 * inverse, total2 * weight2 * inverse
+
+    def first_pass(r, qn, grad, keys, values):
+        scores = [dot_nt(qn, key) for key in keys]
+        top = functools.reduce(jnp.maximum, [jnp.max(s, axis=1, keepdims=True) for s in scores])
+        expo = [jnp.exp2((s - top) * power) for s in scores]
+        total = functools.reduce(jnp.add, [jnp.sum(e, axis=1, keepdims=True) for e in expo])
+        summed = functools.reduce(jnp.add, [dot_nn(e.astype(BF16), val) for e, val in zip(expo, values)])
+        near_trip[r, :, 0:1] = top
+        near_trip[r, :, 1:2] = total
+        near_trip[r, :, 2:3] = jnp.sum(grad.astype(F32) * summed, axis=1, keepdims=True)
+        return summed, total
+
+    def second_pass(qn, grad, keys, values, top, inverse, delta):
+        probs = [jnp.exp2((dot_nt(qn, key) - top) * power) * inverse for key in keys]
+        grad_scores = [(p * (dot_nt(grad, val) - delta)).astype(BF16) for p, val in zip(probs, values)]
+        grad_qn = functools.reduce(jnp.add, [dot_nn(s, key) for s, key in zip(grad_scores, keys)]) * scaling
+        return probs[0], grad_scores[0], grad_qn
+
+    def trade(target):
+        lane = lax.broadcasted_iota(jnp.int32, (length, DH), 1)
+        packed = jnp.zeros((length, DH), F32)
+        for r in range(lent):
+            for i in range(3):
+                packed = jnp.where(lane == 3 * r + i, near_trip[r, :, i : i + 1], packed)
+        trip_out[...] = jnp.transpose(packed)[: trip_out.shape[0]]
+        trip_copy(target).start()
+
+    def traded(target):
+        trip_copy(target).wait_recv()
+        unpacked = jnp.transpose(trip_in[...])
+        for r in range(lent):
+            for i in range(3):
+                far_trip[r, :, i : i + 1] = unpacked[:, 3 * r + i : 3 * r + i + 1]
+
+    def far_operands(r):
+        cols = columns(kept + r)
+        q_full = far_q[r].astype(F32)
+        rate, gain = far_rates[:, 0:1], gq[:, cols]
+        keys = [cks[j, :, cols] for j in range(2)]
+        values = [cvs[j, :, cols] for j in range(2)]
+        return cols, q_full, rate, gain, (q_full * rate * gain).astype(BF16), far_g[r], keys, values
+
+    def near_operands(nb, r):
+        cols = columns(kept + r)
+        q_full = q[:, cols].astype(F32)
+        k_full = k[:, cols].astype(F32)
+        qn = (q_full * rates[:, 0:1] * gq[:, cols]).astype(BF16)
+        kn = (k_full * rates[:, 1:2] * gk[:, cols]).astype(BF16)
+        keys = [kn] + [cks[j, :, cols] for j in range(2, nb)]
+        values = [v[:, cols]] + [cvs[j, :, cols] for j in range(2, nb)]
+        return cols, q_full, k_full, qn, g[:, cols], keys, values
+
+    def help_first(nb, r):
+        for kind in range(2):
+            far_copy(kind, r, nb).wait_recv()
+        if nb == 0:
+            for kv in range(2):
+                clean_copy(1, kept + r, kv, 1, own_send.at[1]).wait_recv()
+        _, _, _, _, qn, grad, keys, values = far_operands(r)
+        summed, total = first_pass(r, qn, grad, keys, values)
+        back_out[1, r] = (summed / total).astype(BF16)
+
+    def help_second(r):
+        cols, q_full, rate, gain, qn, grad, keys, values = far_operands(r)
+        top, inverse, delta, _, _ = merged(near_trip[r], far_trip[r])
+        _, _, grad_qn = second_pass(qn, grad, keys, values, top, inverse, delta)
+        back_out[0, r] = grad_qn.astype(BF16)
+        far_inner[...] += q_full * (grad_qn * gain)
+        sums1[me1, 0:1, cols] += jnp.sum(grad_qn * q_full * rate, axis=0, keepdims=True)
+
+    def near_first(nb, r):
+        for j in range(2, nb):
+            for kv in range(2):
+                clean_copy(j, kept + r, kv, j, own_send.at[1]).wait_recv()
+        _, _, _, qn, grad, keys, values = near_operands(nb, r)
+        part[r] = first_pass(r, qn, grad, keys, values)[0]
+
+    def near_second(nb, r):
+        cols, q_full, k_full, qn, grad, keys, values = near_operands(nb, r)
+        top, inverse, delta, near, far = merged(near_trip[r], far_trip[r])
+        part[r] = part[r] * near
+        far_trip[r, :, 3:4] = far
+        probs, grad_scores, grad_qn = second_pass(qn, grad, keys, values, top, inverse, delta)
+        grad_kn = dot_tn(grad_scores, qn) * scaling
+        dv_out[:, cols] = dot_tn(probs.astype(BF16), grad).astype(BF16)
+        store_grads(cols, q_full, k_full, grad_qn, grad_kn)
 
     for nb in range(frames):
 
         @pl.when(frame == nb)
         def _():
-            def step(h, _):
-                head_step(nb, h)
-                return 0
-
-            lax.fori_loop(0, head_count, step, 0)
-
-    stats_go(1, as_rows(inner_q[...], inner_k[...]))
+            if helps(nb):
+                repeat(0, head_count, functools.partial(head_step, nb))
+                row_copy(nb + 2).wait_recv()
+                far_rates[...] = jnp.transpose(row_in[...])
+                repeat(0, lent, functools.partial(help_first, nb))
+                trade(nb + 2)
+                send_own(nb, kept - 1, [(0, nb + 2)])
+                far_inner[...] = jnp.zeros_like(far_inner)
+                traded(nb + 2)
+                repeat(0, lent, help_second)
+                row_out[...] = as_rows(far_inner[...], jnp.zeros_like(far_inner))
+                row_copy(nb + 2).start()
+                stats_go(1, as_rows(inner_q[...], inner_k[...]))
+            elif helped(nb):
+                repeat(0, lent, functools.partial(near_first, nb))
+                trade(nb - 2)
+                repeat(0, kept - 1, functools.partial(head_step, nb))
+                traded(nb - 2)
+                repeat(0, lent, functools.partial(near_second, nb))
+                repeat(kept - 1, kept, functools.partial(head_step, nb))
+                row_copy(nb - 2).wait_recv()
+                stats_go(1, as_rows(inner_q[...], inner_k[...]) + row_in[...])
+            else:
+                repeat(0, head_count, functools.partial(head_step, nb))
+                stats_go(1, as_rows(inner_q[...], inner_k[...]))
 
     def s1_copy(d, slot):
         return pltpu.make_async_remote_copy(
@@ -257,6 +461,13 @@
         return 0
 
     lax.fori_loop(1, n1, s1_go, 0)
+    for nb in range(frames):
+        if helps(nb):
+
+            @pl.when(frame == nb)
+            def _():
+                for kind in range(2):
+                    repeat(0, lent, lambda r: back_copy(kind, r, nb + 2).start())
 
     inners = jnp.transpose(stats_total(1))
     rate_q = rates[:, 0:1]
@@ -279,13 +490,38 @@
         dk_out[:, cols] = (rate_k * flat_k[:, cols] - k[:, cols].astype(F32) * cube_k).astype(BF16)
         return 0
 
-    lax.fori_loop(0, head_count, finish, 0)
+    lax.fori_loop(0, kept, finish, 0)
+    for nb in range(frames):
+        if helped(nb):
+
+            @pl.when(frame == nb)
+            def _():
+                def add(r):
+                    cols = columns(kept + r)
+                    back_copy(0, r, nb - 2).wait_recv()
+                    flat_q[:, cols] += back_in[0, r].astype(F32) * gq[:, cols]
+
+                repeat(0, lent, add)
+
+    lax.fori_loop(kept, head_count, finish, 0)
     for d in range(1, n2):
         s2_copy(d, lax.rem(me2 + n2 - d, n2)).wait_recv()
     for p in range(n2):
         gain_q_out[:, p * width : (p + 1) * width] = sums2[p, 0:1, :]
         gain_k_out[:, p * width : (p + 1) * width] = sums2[p, 1:2, :]
 
+    for nb in range(frames):
+        if helped(nb):
+
+            @pl.when(frame == nb)
+            def _():
+                def join(r):
+                    back_copy(1, r, nb - 2).wait_recv()
+                    far = back_in[1, r].astype(F32) * far_trip[r, :, 3:4]
+                    att_out[:, columns(kept + r)] = (part[r] + far).astype(BF16)
+
+                repeat(0, lent, join)
+
     for d in range(1, n2):
         stats_copy(0, d, me2).wait_send()
         stats_copy(1, d, me2).wait_send()
@@ -297,20 +533,31 @@
 
     lax.fori_loop(1, n1, s1_gone, 0)
     for nb in range(frames):
-        direct, _, own, passes = plan(nb)
+        direct, _, _, passes = plan(nb)
+        full, _, lends = own_lists(nb)
 
         @pl.when(frame == nb)
         def _():
-            def gone(h, _):
-                for kv in range(2):
-                    for t, target in enumerate(own):
-                        clean_copy(nb, h, kv, target, own_send.at[t], True).wait_send()
-                    for j in direct:
-                        for t, target in enumerate(passes):
-                            clean_copy(j, h, kv, target, relay_send.at[t, j], False).wait_send()
-                return 0
-
-            lax.fori_loop(0, head_count, gone, 0)
+            def gone(targets, relays):
+                def step(h):
+                    for kv in range(2):
+                        for t, target in targets:
+                            clean_copy(nb, h, kv, target, own_send.at[t]).wait_send()
+                        for j in relays:
+                            for t, target in enumerate(passes):
+                                clean_copy(j, h, kv, target, relay_send.at[t, j]).wait_send()
+
+                return step
+
+            repeat(0, kept, gone(full, direct))
+            repeat(kept, head_count, gone(lends, []))
+            if helps(nb) or helped(nb):
+                other = nb + 2 if helps(nb) else nb - 2
+                trip_copy(other).wait_send()
+                row_copy(other).wait_send()
+                copy = back_copy if helps(nb) else far_copy
+                for kind in range(2):
+                    repeat(0, lent, lambda r: copy(kind, r, other).wait_send())
 
 
 def write_out(*refs):
@@ -338,8 +585,11 @@
     dma = pltpu.SemaphoreType.DMA
     earlier = max(frames - 1, 1)
     kept = 4 * 2 * length * width + 2 * 4 * features
+    lent = head_count * 2 // 5 if frames == 4 else 0
+    held = max(lent, 1)
+    trip_rows = -(-3 * held // 8) * 8
     outs = pl.pallas_call(
-        functools.partial(kernel, frames, fsdp, heads_axis, width, features),
+        functools.partial(kernel, frames, fsdp, heads_axis, width, features, lent),
         out_shape=(block, block, block, block, gains, gains),
         in_specs=[anywhere] * 8,
         out_specs=[vmem] * 6,
@@ -350,8 +600,8 @@
             pltpu.VMEM((length, width), BF16),
             pltpu.VMEM((1, width), F32),
             pltpu.VMEM((1, width), F32),
-            pltpu.VMEM((earlier, length, width), BF16),
-            pltpu.VMEM((earlier, length, width), BF16),
+            pltpu.VMEM((frames, length, width), BF16),
+            pltpu.VMEM((frames, length, width), BF16),
             pltpu.VMEM((length, width), F32),
             pltpu.VMEM((length, width), F32),
             pltpu.VMEM((length, DH), F32),
@@ -360,16 +610,38 @@
             pltpu.VMEM((2, n2, 8, length), F32),
             pltpu.VMEM((n1, 2, width), F32),
             pltpu.VMEM((n2, 2, width), F32),
+            pltpu.VMEM((held, length, DH), BF16),
+            pltpu.VMEM((held, length, DH), BF16),
+            pltpu.VMEM((length, 8), F32),
+            pltpu.VMEM((length, DH), F32),
+            pltpu.VMEM((held, length, DH), F32),
+            pltpu.VMEM((2, held, length, DH), BF16),
+            pltpu.VMEM((2, held, length, DH), BF16),
+            pltpu.VMEM((held, length, 8), F32),
+            pltpu.VMEM((held, length, 8), F32),
+            pltpu.VMEM((trip_rows, length), F32),
+            pltpu.VMEM((trip_rows, length), F32),
+            pltpu.VMEM((8, length), F32),
+            pltpu.VMEM((8, length), F32),
             dma((6,)),
             dma((2, head_count, 2)),
             dma((2, earlier, head_count, 2)),
-            dma((earlier, head_count, 2)),
+            dma((frames, head_count, 2)),
             dma((2, n2)),
             dma((2, n2)),
             dma((n1,)),
             dma((n1,)),
             dma((n2,)),
             dma((n2,)),
+            dma((head_count, 2)),
+            dma((2, held)),
+            dma((2, held)),
+            dma((2, held)),
+            dma((2, held)),
+            dma((1,)),
+            dma((1,)),
+            dma((1,)),
+            dma((1,)),
         ],
         compiler_params=pltpu.CompilerParams(
             collective_id=0, has_side_effects=True, vmem_limit_bytes=VMEM_BYTES - kept - 4096

time: 50.5 us -> 44.3 us (0.88)
  Pallas kernels: 49.7 us -> 43.3 us
    pallas_call x1, Pallas kernels: 48.1 us -> 41.8 us  [on_device(): pl.pallas_call(functools.partial(kernel, frames, fsdp, heads_axis, width,...]
where the time goes in v1:
time: 44.3 us; the launch traced here: 44.1 us
  Pallas kernels  43.3 us (98%)
  between operations  0.8 us (2%)
    pallas_call x1, Pallas kernels, on_device(): pl.pallas_call(functools.partial(kernel, frames, fsdp, heads_axis, width,...  41.8 us
    pallas_call x1, Pallas kernels, on_device(): pl.pallas_call(write_out, out_shape=tuple((jax.ShapeDtypeStruct(out.shape...  1.54 us

profile of v1, /device:TPU:0, one launch (start us, length us, event | category | flops | bytes accessed | tf_op | source)
XLA Modules:
  0.0 44.1 jit_solution(1395028863959679771)
XLA Ops:
  0.6 41.8 %attention.1 = (bf16[256,1280]{1,0:T(8,128)(2,1)S(1)}, bf16[256,1280]{1,0:T(8,128)(2,1)S(1)}, bf16[256,1280]{1,0:T(8,128)(2,1)S(1)}, bf16[256,1280]{1,0:T(8,128)...) custom-call(bf16[256,1280]{1,0:T(8,128)(2,1)} %q_hbm.1, bf16[256,1280]{1,0:T(8,128)(2,1)} %k_hbm.1, ...), custom_call_target="tpu_custom_call" | custom-call | tf_op jit(solution)/shard_map/attention/pallas_call | solution.py:591
  42.4 1.5 %write_out.1 = (bf16[256,1280]{1,0:T(8,128)(2,1)}, bf16[256,1280]{1,0:T(8,128)(2,1)}, bf16[256,1280]{1,0:T(8,128)(2,1)}, bf16[256,1280]{1,0:T(8,128)(2,1)}, f32[1,5120]{1,0:T(1,128)}, /*index=5*/f32[1,5120]{1,0:T(1,128)}) custom-call(bf16[256,1280]{1,0:T(8,128)(2,1)S(1)} %get-tuple-element.18.refs_0_, bf16[256,1280]{1,0:T(8,128)(2,1)S(1)} %get-tuple-element.19.refs_1_, ...), custom_call_target="tpu_custom_call" | custom-call | tf_op jit(solution)/shard_map/write_out/pallas_call | solution.py:654

commit v2 on v1

v2 whole, which is shorter than its diff:
```python
import functools
import math

import jax
import jax.numpy as jnp
from jax import lax
from jax.experimental import pallas as pl
from jax.experimental.pallas import tpu as pltpu
from jax.sharding import PartitionSpec as P

DH = 128
EPSILON = 1e-06
MESH = pl.DeviceIdType.MESH
VMEM_BYTES = 67043328
F32 = jnp.float32
BF16 = jnp.bfloat16


def dot_nt(a, b):
    return lax.dot_general(a, b, (((1,), (1,)), ((), ())), preferred_element_type=F32)


def dot_nn(a, b):
    return lax.dot_general(a, b, (((1,), (0,)), ((), ())), preferred_element_type=F32)


def dot_tn(a, b):
    return lax.dot_general(a, b, (((0,), (0,)), ((), ())), preferred_element_type=F32)


def kernel(
    frames, fsdp, heads_axis, width, features, lent,
    q_hbm, k_hbm, v_hbm, ck_hbm, cv_hbm, gq_hbm, gk_hbm, g_hbm,
    att_out, dq_out, dk_out, dv_out, gain_q_out, gain_k_out,
    tokens, gains, clean, flat_q, flat_k, inner_q, inner_k, rates,
    stats, sums1, sums2, far, far_rates, far_inner, far_sums, part, back_out, back_in,
    near_trip, far_trip, trip_out, trip_in, row_out, row_in,
    load_sem, own_send, relay_send, direct_recv, relay_recv, partner_recv, stats_send, stats_recv, sum_send, sum_recv,
    far_send, far_recv, back_send, grad_recv, att_recv, row_send, row_recv,
):
    q, k, v, g = [tokens.at[i] for i in range(4)]
    gq, gk = gains.at[0], gains.at[1]
    length = tokens.shape[1]
    head_count = width // DH
    kept = head_count - lent
    videos = fsdp // 2
    scaling = 1.0 / math.sqrt(DH)
    power = scaling * math.log2(math.e)
    frame = lax.axis_index("frame")
    fs = lax.axis_index("fsdp")
    half = fs // videos
    video = lax.rem(fs, videos)
    me1 = frame * videos + video
    n1 = frames * videos
    me2 = half * heads_axis + lax.axis_index("head")
    n2 = 2 * heads_axis

    def peer1(distance):
        p = lax.rem(me1 + distance, n1)
        return {"frame": p // videos, "fsdp": half * videos + lax.rem(p, videos)}

    def peer2(distance):
        p = lax.rem(me2 + distance, n2)
        return {"fsdp": (p // heads_axis) * videos + video, "head": lax.rem(p, heads_axis)}

    def columns(h):
        return pl.ds(pl.multiple_of(h * DH, DH), DH)

    def repeat(first, last, step):
        def body(i, _):
            step(i)
            return 0

        lax.fori_loop(first, last, body, 0)

    def arrive(ref, sem):
        pltpu.make_async_copy(ref, ref, sem).wait()

    for nb in range(frames - 1):

        @pl.when(frame == nb)
        def _():
            for kv, src in enumerate((ck_hbm, cv_hbm)):
                pltpu.make_async_copy(src, clean.at[nb, kv], load_sem.at[3]).start()

    barrier = pltpu.get_barrier_semaphore()

    def greet(d, _):
        pl.semaphore_signal(barrier, inc=1, device_id=peer1(d), device_id_type=MESH)
        return 0

    lax.fori_loop(1, n1, greet, 0)
    for d in range(1, n2):
        pl.semaphore_signal(barrier, inc=1, device_id=peer2(d), device_id_type=MESH)
    start = pl.multiple_of(me2 * width, DH)
    for src, dst, i in (
        (q_hbm, q, 0),
        (k_hbm, k, 0),
        (gq_hbm.at[:, pl.ds(start, width)], gq, 1),
        (gk_hbm.at[:, pl.ds(start, width)], gk, 1),
        (v_hbm, v, 2),
        (g_hbm, g, 2),
    ):
        pltpu.make_async_copy(src, dst, load_sem.at[i]).start()
    pl.semaphore_wait(barrier, n1 - 1 + n2 - 1)

    def frame_copy(src, dst, send, recv, target):
        return pltpu.make_async_remote_copy(
            src_ref=src,
            dst_ref=dst,
            send_sem=send,
            recv_sem=recv,
            device_id={"frame": jnp.int32(target)},
            device_id_type=MESH,
        )

    def direct_copy(j, h, target, send):
        land = clean.at[j, :, :, columns(h)]
        return frame_copy(land, land, send, direct_recv.at[j // 2, h], target)

    def relay_copy(j, h, target, send):
        land = clean.at[j, :, :, columns(h)]
        return frame_copy(land, land, send, relay_recv.at[j // 2, h], target)

    def partner_copy(j):
        land = clean.at[j] if j % 2 == 0 else clean.at[j, :, :, pl.ds(kept * DH, lent * DH)]
        return frame_copy(land, land, own_send.at[1], partner_recv.at[0], 2 * (j // 2) + 1 - j % 2)

    def kept_heads(j, sem):
        land = clean.at[j, :, :, pl.ds(0, kept * DH)]
        return frame_copy(land, land, sem, partner_recv.at[0], (j + 1) % frames)

    def plan(nb):
        pair, side = nb // 2, nb % 2
        partner, further = 2 * pair + 1 - side, nb + 2
        direct = [2 * c + side for c in range(pair)]
        relayed = [2 * c + 1 - side for c in range(pair)]
        return direct, relayed, partner, further if further < frames else None

    def helps(nb):
        return lent > 0 and nb < 2

    def helped(nb):
        return lent > 0 and nb >= 2

    def has_partner_copy(nb):
        return nb % 2 == 0 or helps(nb)

    def send_own(nb, first, last):
        further = plan(nb)[3]
        repeat(first, last, lambda h: direct_copy(nb, h, further, own_send.at[0]).start())

    def far_copy(kind, r, target):
        src = (q_hbm, g_hbm)[kind].at[:, columns(kept + r)]
        return frame_copy(src, far.at[r, kind], far_send.at[0], far_recv.at[r], target)

    def back_copy(kind, r, target):
        recv = grad_recv.at[0] if kind == 0 else att_recv.at[r]
        return frame_copy(back_out.at[kind, r], back_in.at[kind, r], back_send.at[0], recv, target)

    def trip_copy(target):
        return frame_copy(trip_out, trip_in, row_send.at[1], row_recv.at[1], target)

    def row_copy(target):
        return frame_copy(row_out, row_in, row_send.at[0], row_recv.at[0], target)

    def lend(nb, first, last):
        def go(r):
            for kind in range(2):
                far_copy(kind, r, nb - 2).start()

        repeat(first, last, go)

    for nb in range(frames):

        @pl.when(frame == nb)
        def _():
            if helped(nb):
                lend(nb, 0, lent // 2)
            if nb < frames - 1:
                arrive(clean.at[nb], load_sem.at[3])
            if plan(nb)[3] is not None:
                send_own(nb, 0, kept - 1 if helps(nb) else kept)
            if has_partner_copy(nb):
                partner_copy(nb).start()

    row = lax.broadcasted_iota(jnp.int32, (8, length), 0)

    def as_rows(a, b):
        a = jnp.sum(jnp.transpose(a), axis=0, keepdims=True)
        b = jnp.sum(jnp.transpose(b), axis=0, keepdims=True)
        return jnp.where(row == 0, a, jnp.where(row == 1, b, 0.0))

    def stats_copy(phase, d, part):
        return pltpu.make_async_remote_copy(
            src_ref=part,
            dst_ref=part,
            send_sem=stats_send.at[phase],
            recv_sem=stats_recv.at[phase],
            device_id=peer2(d),
            device_id_type=MESH,
        )

    def all_stats(phase):
        return stats_copy(phase, 1, stats.at[phase, pl.ds(0, n2 - 1)])

    def stats_go(phase, value):
        stats[phase, me2] = value
        for d in range(1, n2):
            stats_copy(phase, d, stats.at[phase, me2]).start()

    def stats_total(phase):
        all_stats(phase).wait_recv()
        return jnp.sum(stats[phase], axis=0)

    arrive(tokens.at[pl.ds(0, 2)], load_sem.at[0])

    def square(ref):
        total = jnp.zeros((length, DH), F32)
        for h in range(head_count):
            x = ref[:, h * DH : (h + 1) * DH].astype(F32)
            total = total + x * x
        return total

    stats_go(0, as_rows(square(q), square(k)))
    inner_q[...] = jnp.zeros_like(inner_q)
    inner_k[...] = jnp.zeros_like(inner_k)
    arrive(gains, load_sem.at[1])
    arrive(tokens.at[pl.ds(2, 2)], load_sem.at[2])
    rate_rows = lax.rsqrt(stats_total(0) / features + EPSILON)
    rates[...] = jnp.transpose(rate_rows)
    for nb in range(frames):
        if helped(nb):

            @pl.when(frame == nb)
            def _():
                row_out[...] = rate_rows
                row_copy(nb - 2).start()
                lend(nb, lent // 2, lent)

    def store_grads(cols, q_full, k_full, grad_qn, grad_kn):
        fq = grad_qn * gq[:, cols]
        fk = grad_kn * gk[:, cols]
        flat_q[:, cols] = fq
        flat_k[:, cols] = fk
        inner_q[...] += q_full * fq
        inner_k[...] += k_full * fk
        sums1[me1, 0:1, cols] = jnp.sum(grad_qn * q_full * rates[:, 0:1], axis=0, keepdims=True)
        sums1[me1, 1:2, cols] = jnp.sum(grad_kn * k_full * rates[:, 1:2], axis=0, keepdims=True)

    def head_step(nb, h):
        direct, relayed, partner, further = plan(nb)
        cols = columns(h)
        for j in direct:
            direct_copy(j, h, partner, relay_send.at[0, j // 2]).wait_recv()
            relay_copy(j, h, partner, relay_send.at[0, j // 2]).start()
            if further is not None:
                direct_copy(j, h, further, relay_send.at[1, j // 2]).start()
        rate_q = rates[:, 0:1]
        rate_k = rates[:, 1:2]
        q_full = q[:, cols].astype(F32)
        k_full = k[:, cols].astype(F32)
        gain_q = gq[:, cols]
        gain_k = gk[:, cols]
        qn = (q_full * rate_q * gain_q).astype(BF16)
        kn = (k_full * rate_k * gain_k).astype(BF16)
        val = v[:, cols]
        grad = g[:, cols]
        scores = [dot_nt(qn, kn)]
        grad_probs = [dot_nt(grad, val)]
        for j in relayed:
            relay_copy(j, h, partner, relay_send.at[0, j // 2]).wait_recv()
        for j in range(nb):
            scores.append(dot_nt(qn, clean[j, 0, :, cols]))
            grad_probs.append(dot_nt(grad, clean[j, 1, :, cols]))
        top = functools.reduce(jnp.maximum, [jnp.max(s, axis=1, keepdims=True) for s in scores])
        expo = [jnp.exp2((s - top) * power) for s in scores]
        total = functools.reduce(jnp.add, [jnp.sum(e, axis=1, keepdims=True) for e in expo])
        summed = dot_nn(expo[0].astype(BF16), val)
        for j in range(nb):
            summed = summed + dot_nn(expo[j + 1].astype(BF16), clean[j, 1, :, cols])
        inverse = 1.0 / total
        attention = summed * inverse
        att_out[:, cols] = attention.astype(BF16)
        delta = jnp.sum(grad.astype(F32) * attention, axis=1, keepdims=True)
        probs = [e * inverse for e in expo]
        grad_scores = [(p * (d - delta)).astype(BF16) for p, d in zip(probs, grad_probs)]
        grad_qn = dot_nn(grad_scores[0], kn)
        for j in range(nb):
            grad_qn = grad_qn + dot_nn(grad_scores[j + 1], clean[j, 0, :, cols])
        grad_qn = grad_qn * scaling
        grad_kn = dot_tn(grad_scores[0], qn) * scaling
        dv_out[:, cols] = dot_tn(probs[0].astype(BF16), grad).astype(BF16)
        store_grads(cols, q_full, k_full, grad_qn, grad_kn)

    def merged(mine, theirs):
        top1, total1, dot1 = [mine[:, i : i + 1] for i in range(3)]
        top2, total2, dot2 = [theirs[:, i : i + 1] for i in range(3)]
        top = jnp.maximum(top1, top2)
        weight1 = jnp.exp2((top1 - top) * power)
        weight2 = jnp.exp2((top2 - top) * power)
        inverse = 1.0 / (total1 * weight1 + total2 * weight2)
        delta = (dot1 * weight1 + dot2 * weight2) * inverse
        return top, inverse, delta, weight1 * inverse, total2 * weight2 * inverse

    def first_pass(r, qn, grad, keys, values):
        scores = [dot_nt(qn, key) for key in keys]
        top = functools.reduce(jnp.maximum, [jnp.max(s, axis=1, keepdims=True) for s in scores])
        expo = [jnp.exp2((s - top) * power) for s in scores]
        total = functools.reduce(jnp.add, [jnp.sum(e, axis=1, keepdims=True) for e in expo])
        summed = functools.reduce(jnp.add, [dot_nn(e.astype(BF16), val) for e, val in zip(expo, values)])
        near_trip[r, :, 0:1] = top
        near_trip[r, :, 1:2] = total
        near_trip[r, :, 2:3] = jnp.sum(grad.astype(F32) * summed, axis=1, keepdims=True)
        return summed, total

    def second_pass(qn, grad, keys, values, top, inverse, delta):
        probs = [jnp.exp2((dot_nt(qn, key) - top) * power) * inverse for key in keys]
        grad_scores = [(p * (dot_nt(grad, val) - delta)).astype(BF16) for p, val in zip(probs, values)]
        grad_qn = functools.reduce(jnp.add, [dot_nn(s, key) for s, key in zip(grad_scores, keys)]) * scaling
        return probs[0], grad_scores[0], grad_qn

    def trade(target):
        lane = lax.broadcasted_iota(jnp.int32, (length, DH), 1)
        packed = jnp.zeros((length, DH), F32)
        for r in range(lent):
            for i in range(3):
                packed = jnp.where(lane == 3 * r + i, near_trip[r, :, i : i + 1], packed)
        trip_out[...] = jnp.transpose(packed)[: trip_out.shape[0]]
        trip_copy(target).start()

    def traded(target):
        trip_copy(target).wait_recv()
        unpacked = jnp.transpose(trip_in[...])
        for r in range(lent):
            for i in range(3):
                far_trip[r, :, i : i + 1] = unpacked[:, 3 * r + i : 3 * r + i + 1]

    def far_operands(r):
        cols = columns(kept + r)
        q_full = far[r, 0].astype(F32)
        rate, gain = far_rates[:, 0:1], gq[:, cols]
        keys = [clean[j, 0, :, cols] for j in range(2)]
        values = [clean[j, 1, :, cols] for j in range(2)]
        return cols, q_full, rate, gain, (q_full * rate * gain).astype(BF16), far[r, 1], keys, values

    def near_operands(nb, r):
        cols = columns(kept + r)
        q_full = q[:, cols].astype(F32)
        k_full = k[:, cols].astype(F32)
        qn = (q_full * rates[:, 0:1] * gq[:, cols]).astype(BF16)
        kn = (k_full * rates[:, 1:2] * gk[:, cols]).astype(BF16)
        keys = [kn] + [clean[j, 0, :, cols] for j in range(2, nb)]
        values = [v[:, cols]] + [clean[j, 1, :, cols] for j in range(2, nb)]
        return cols, q_full, k_full, qn, g[:, cols], keys, values

    def help_first(nb, r):
        frame_copy(far.at[r], far.at[r], far_send.at[0], far_recv.at[r], nb + 2).wait_recv()
        _, _, _, _, qn, grad, keys, values = far_operands(r)
        summed, total = first_pass(r, qn, grad, keys, values)
        back_out[1, r] = (summed / total).astype(BF16)

    def help_second(r):
        cols, q_full, rate, gain, qn, grad, keys, values = far_operands(r)
        top, inverse, delta, _, _ = merged(near_trip[r], far_trip[r])
        _, _, grad_qn = second_pass(qn, grad, keys, values, top, inverse, delta)
        back_out[0, r] = grad_qn.astype(BF16)
        far_inner[...] += q_full * (grad_qn * gain)
        far_sums[pl.ds(r, 1), :] = jnp.sum(grad_qn * q_full * rate, axis=0, keepdims=True)

    def near_first(nb, r):
        _, _, _, qn, grad, keys, values = near_operands(nb, r)
        part[r] = first_pass(r, qn, grad, keys, values)[0]

    def near_second(nb, r):
        cols, q_full, k_full, qn, grad, keys, values = near_operands(nb, r)
        top, inverse, delta, near, far = merged(near_trip[r], far_trip[r])
        part[r] = part[r] * near
        far_trip[r, :, 3:4] = far
        probs, grad_scores, grad_qn = second_pass(qn, grad, keys, values, top, inverse, delta)
        grad_kn = dot_tn(grad_scores, qn) * scaling
        dv_out[:, cols] = dot_tn(probs.astype(BF16), grad).astype(BF16)
        store_grads(cols, q_full, k_full, grad_qn, grad_kn)

    for nb in range(frames):

        @pl.when(frame == nb)
        def _():
            own = functools.partial(head_step, nb)
            if nb % 2 == 1:
                partner_copy(nb - 1).wait_recv()
            if helps(nb):
                first, middle = head_count * 3 // 10, head_count // 2
                repeat(0, first, own)
                if nb == 0:
                    partner_copy(1).wait_recv()
                row_copy(nb + 2).wait_recv()
                far_rates[...] = jnp.transpose(row_in[...])
                repeat(0, lent // 2, functools.partial(help_first, nb))
                repeat(first, middle, own)
                repeat(lent // 2, lent, functools.partial(help_first, nb))
                trade(nb + 2)
                send_own(nb, kept - 1, kept)
                far_inner[...] = jnp.zeros_like(far_inner)
                traded(nb + 2)
                repeat(0, lent, help_second)
                row_out[...] = as_rows(far_inner[...], jnp.zeros_like(far_inner))
                row_copy(nb + 2).start()
                repeat(0, lent, lambda r: back_copy(0, r, nb + 2).start())
                repeat(middle, head_count, own)
                for r in range(lent):
                    cols = columns(kept + r)
                    sums1[me1, 0:1, cols] += far_sums[r : r + 1, :]
                stats_go(1, as_rows(inner_q[...], inner_k[...]))
            elif helped(nb):
                repeat(0, lent, functools.partial(near_first, nb))
                trade(nb - 2)
                repeat(0, kept - 1, own)
                traded(nb - 2)
                repeat(0, lent, functools.partial(near_second, nb))
                repeat(kept - 1, kept, own)
                row_copy(nb - 2).wait_recv()
                stats_go(1, as_rows(inner_q[...], inner_k[...]) + row_in[...])
            else:
                repeat(0, head_count, own)
                stats_go(1, as_rows(inner_q[...], inner_k[...]))

    def s1_copy(d, part):
        return pltpu.make_async_remote_copy(
            src_ref=part,
            dst_ref=part,
            send_sem=sum_send.at[0],
            recv_sem=sum_recv.at[0],
            device_id=peer1(d),
            device_id_type=MESH,
        )

    def s2_copy(d, part):
        return pltpu.make_async_remote_copy(
            src_ref=part,
            dst_ref=part,
            send_sem=sum_send.at[1],
            recv_sem=sum_recv.at[1],
            device_id=peer2(d),
            device_id_type=MESH,
        )

    all_s1 = s1_copy(1, sums1.at[pl.ds(0, n1 - 1)])
    all_s2 = s2_copy(1, sums2.at[pl.ds(0, n2 - 1)])
    repeat(1, n1, lambda d: s1_copy(d, sums1.at[me1]).start())
    for nb in range(frames):
        if helps(nb):

            @pl.when(frame == nb)
            def _():
                repeat(0, lent, lambda r: back_copy(1, r, nb + 2).start())

    inners = jnp.transpose(stats_total(1))
    rate_q = rates[:, 0:1]
    rate_k = rates[:, 1:2]
    cube_q = rate_q * rate_q * rate_q * inners[:, 0:1] / features
    cube_k = rate_k * rate_k * rate_k * inners[:, 1:2] / features

    all_s1.wait_recv()
    sums2[me2] = jnp.sum(sums1[...], axis=0)
    for d in range(1, n2):
        s2_copy(d, sums2.at[me2]).start()

    def finish(h, _):
        cols = columns(h)
        dq_out[:, cols] = (rate_q * flat_q[:, cols] - q[:, cols].astype(F32) * cube_q).astype(BF16)
        dk_out[:, cols] = (rate_k * flat_k[:, cols] - k[:, cols].astype(F32) * cube_k).astype(BF16)
        return 0

    lax.fori_loop(0, kept, finish, 0)
    for nb in range(frames):
        if helped(nb):

            @pl.when(frame == nb)
            def _():
                grads = back_in.at[0]
                frame_copy(grads, grads, back_send.at[0], grad_recv.at[0], nb - 2).wait_recv()

                def add(r):
                    cols = columns(kept + r)
                    flat_q[:, cols] += back_in[0, r].astype(F32) * gq[:, cols]

                repeat(0, lent, add)

    lax.fori_loop(kept, head_count, finish, 0)
    all_s2.wait_recv()
    for p in range(n2):
        gain_q_out[:, p * width : (p + 1) * width] = sums2[p, 0:1, :]
        gain_k_out[:, p * width : (p + 1) * width] = sums2[p, 1:2, :]

    for nb in range(frames):
        if helped(nb):

            @pl.when(frame == nb)
            def _():
                def join(r):
                    back_copy(1, r, nb - 2).wait_recv()
                    far = back_in[1, r].astype(F32) * far_trip[r, :, 3:4]
                    att_out[:, columns(kept + r)] = (part[r] + far).astype(BF16)

                repeat(0, lent, join)

    all_stats(0).wait_send()
    all_stats(1).wait_send()
    all_s1.wait_send()
    all_s2.wait_send()
    for nb in range(frames):
        direct, _, _, further = plan(nb)

        @pl.when(frame == nb)
        def _():
            if further is not None:
                kept_heads(nb, own_send.at[0]).wait_send()
            if has_partner_copy(nb):
                partner_copy(nb).wait_send()
            for j in direct:
                for t in range(1 if further is None else 2):
                    kept_heads(j, relay_send.at[t, j // 2]).wait_send()
            if helps(nb) or helped(nb):
                other = nb + 2 if helps(nb) else nb - 2
                trip_copy(other).wait_send()
                row_copy(other).wait_send()
            if helps(nb):
                frame_copy(back_out, back_in, back_send.at[0], grad_recv.at[0], nb + 2).wait_send()
            if helped(nb):
                frame_copy(far, far, far_send.at[0], far_recv.at[0], nb - 2).wait_send()


def write_out(*refs):
    sem = refs[12]
    copies = [pltpu.make_async_copy(refs[i], refs[6 + i], sem.at[i]) for i in range(6)]
    for copy in copies:
        copy.start()
    for copy in copies:
        copy.wait()


def on_device(queries, noisy_keys, noisy_values, clean_keys, clean_values, gain_query, gain_key, out_grad):
    length, width = queries.shape
    features = gain_query.shape[0]
    frames = lax.axis_size("frame")
    fsdp = lax.axis_size("fsdp")
    heads_axis = lax.axis_size("head")
    head_count = width // DH
    n1 = frames * (fsdp // 2)
    n2 = 2 * heads_axis
    block = pltpu.VMEM((length, width), BF16)
    gains = pltpu.VMEM((1, features), F32)
    anywhere = pl.BlockSpec(memory_space=pl.ANY)
    vmem = pl.BlockSpec(memory_space=pltpu.VMEM)
    dma = pltpu.SemaphoreType.DMA
    chips = max(frames // 2 - 1, 1)
    kept = 4 * 2 * length * width + 2 * 4 * features
    lent = head_count * 2 // 5 if frames == 4 else 0
    held = max(lent, 1)
    kept_count = head_count - lent
    trip_rows = -(-3 * held // 8) * 8
    outs = pl.pallas_call(
        functools.partial(kernel, frames, fsdp, heads_axis, width, features, lent),
        out_shape=(block, block, block, block, gains, gains),
        in_specs=[anywhere] * 8,
        out_specs=[vmem] * 6,
        scratch_shapes=[
            pltpu.VMEM((4, length, width), BF16),
            pltpu.VMEM((2, 1, width), F32),
            pltpu.VMEM((frames, 2, length, width), BF16),
            pltpu.VMEM((length, width), F32),
            pltpu.VMEM((length, width), F32),
            pltpu.VMEM((length, DH), F32),
            pltpu.VMEM((length, DH), F32),
            pltpu.VMEM((length, 8), F32),
            pltpu.VMEM((2, n2, 8, length), F32),
            pltpu.VMEM((n1, 2, width), F32),
            pltpu.VMEM((n2, 2, width), F32),
            pltpu.VMEM((held, 2, length, DH), BF16),
            pltpu.VMEM((length, 8), F32),
            pltpu.VMEM((length, DH), F32),
            pltpu.VMEM((-(-held // 8) * 8, DH), F32),
            pltpu.VMEM((held, length, DH), F32),
            pltpu.VMEM((2, held, length, DH), BF16),
            pltpu.VMEM((2, held, length, DH), BF16),
            pltpu.VMEM((held, length, 8), F32),
            pltpu.VMEM((held, length, 8), F32),
            pltpu.VMEM((trip_rows, length), F32),
            pltpu.VMEM((trip_rows, length), F32),
            pltpu.VMEM((8, length), F32),
            pltpu.VMEM((8, length), F32),
            dma((4,)),
            dma((2,)),
            dma((2, chips)),
            dma((chips, kept_count)),
            dma((chips, kept_count)),
            dma((1,)),
            dma((2,)),
            dma((2,)),
            dma((2,)),
            dma((2,)),
            dma((1,)),
            dma((held,)),
            dma((1,)),
            dma((1,)),
            dma((held,)),
            dma((2,)),
            dma((2,)),
        ],
        compiler_params=pltpu.CompilerParams(
            collective_id=0, has_side_effects=True, vmem_limit_bytes=VMEM_BYTES - kept - 4096
        ),
        name="attention",
    )(
        queries, noisy_keys, noisy_values, clean_keys, clean_values,
        gain_query.reshape(1, features), gain_key.reshape(1, features), out_grad,
    )
    outs = pl.pallas_call(
        write_out,
        out_shape=tuple(jax.ShapeDtypeStruct(out.shape, out.dtype) for out in outs),
        in_specs=[anywhere] * 6,
        out_specs=[anywhere] * 6,
        scratch_shapes=[dma((6,))],
        compiler_params=pltpu.CompilerParams(vmem_limit_bytes=8 * 1024 * 1024),
        name="write_out",
    )(*outs)
    return (*outs[:4], outs[4].reshape(features), outs[5].reshape(features))


def solution(mesh):
    tokens = P("frame", ("fsdp", "head"))
    return jax.shard_map(
        on_device,
        mesh=mesh,
        in_specs=(tokens, tokens, tokens, tokens, tokens, P(), P(), tokens),
        out_specs=(tokens, tokens, tokens, tokens, P(), P()),
        check_vma=False,
    )
```

time: 44.3 us -> 40.7 us (0.919)
  Pallas kernels: 43.3 us -> 39.7 us
    pallas_call x1, Pallas kernels: 41.8 us -> 38.2 us  [on_device(): pl.pallas_call(functools.partial(kernel, frames, fsdp, heads_axis, width,...]
where the time goes in v2:
time: 40.7 us; the launch traced here: 40.5 us
  Pallas kernels  39.7 us (98%)
  between operations  0.8 us (2%)
    pallas_call x1, Pallas kernels, on_device(): pl.pallas_call(functools.partial(kernel, frames, fsdp, heads_axis, width,...  38.2 us
    pallas_call x1, Pallas kernels, on_device(): pl.pallas_call(write_out, out_shape=tuple((jax.ShapeDtypeStruct(out.shape...  1.54 us

profile of v2, /device:TPU:0, one launch (start us, length us, event | category | flops | bytes accessed | tf_op | source)
XLA Modules:
  0.0 40.5 jit_solution(16888722752350649290)
XLA Ops:
  0.6 38.2 %attention.1 = (bf16[256,1280]{1,0:T(8,128)(2,1)S(1)}, bf16[256,1280]{1,0:T(8,128)(2,1)S(1)}, bf16[256,1280]{1,0:T(8,128)(2,1)S(1)}, bf16[256,1280]{1,0:T(8,128)...) custom-call(bf16[256,1280]{1,0:T(8,128)(2,1)} %q_hbm.1, bf16[256,1280]{1,0:T(8,128)(2,1)} %k_hbm.1, ...), custom_call_target="tpu_custom_call" | custom-call | tf_op jit(solution)/shard_map/attention/pallas_call | solution.py:563
  38.8 1.5 %write_out.1 = (bf16[256,1280]{1,0:T(8,128)(2,1)}, bf16[256,1280]{1,0:T(8,128)(2,1)}, bf16[256,1280]{1,0:T(8,128)(2,1)}, bf16[256,1280]{1,0:T(8,128)(2,1)}, f32[1,5120]{1,0:T(1,128)}, /*index=5*/f32[1,5120]{1,0:T(1,128)}) custom-call(bf16[256,1280]{1,0:T(8,128)(2,1)S(1)} %get-tuple-element.18.refs_0_, bf16[256,1280]{1,0:T(8,128)(2,1)S(1)} %get-tuple-element.19.refs_1_, ...), custom_call_target="tpu_custom_call" | custom-call | tf_op jit(solution)/shard_map/write_out/pallas_call | solution.py:619

commit v3 on v2

--- a/solution.py
+++ b/solution.py
@@ -43,6 +43,8 @@
     length = tokens.shape[1]
     head_count = width // DH
     kept = head_count - lent
+    batch = lent // 2
+    group = 2 - head_count % 2
     videos = fsdp // 2
     scaling = 1.0 / math.sqrt(DH)
     power = scaling * math.log2(math.e)
@@ -158,8 +160,8 @@
         recv = grad_recv.at[0] if kind == 0 else att_recv.at[r]
         return frame_copy(back_out.at[kind, r], back_in.at[kind, r], back_send.at[0], recv, target)
 
-    def trip_copy(target):
-        return frame_copy(trip_out, trip_in, row_send.at[1], row_recv.at[1], target)
+    def trip_copy(p, target):
+        return frame_copy(trip_out.at[p], trip_in.at[p], row_send.at[1 + p], row_recv.at[1 + p], target)
 
     def row_copy(target):
         return frame_copy(row_out, row_in, row_send.at[0], row_recv.at[0], target)
@@ -176,11 +178,11 @@
         @pl.when(frame == nb)
         def _():
             if helped(nb):
-                lend(nb, 0, lent // 2)
+                lend(nb, 0, batch)
             if nb < frames - 1:
                 arrive(clean.at[nb], load_sem.at[3])
             if plan(nb)[3] is not None:
-                send_own(nb, 0, kept - 1 if helps(nb) else kept)
+                send_own(nb, 0, kept - 2 if helps(nb) else kept)
             if has_partner_copy(nb):
                 partner_copy(nb).start()
 
@@ -236,7 +238,7 @@
             def _():
                 row_out[...] = rate_rows
                 row_copy(nb - 2).start()
-                lend(nb, lent // 2, lent)
+                lend(nb, batch, lent)
 
     def store_grads(cols, q_full, k_full, grad_qn, grad_kn):
         fq = grad_qn * gq[:, cols]
@@ -248,50 +250,63 @@
         sums1[me1, 0:1, cols] = jnp.sum(grad_qn * q_full * rates[:, 0:1], axis=0, keepdims=True)
         sums1[me1, 1:2, cols] = jnp.sum(grad_kn * k_full * rates[:, 1:2], axis=0, keepdims=True)
 
-    def head_step(nb, h):
-        direct, relayed, partner, further = plan(nb)
-        cols = columns(h)
+    def pass_on(nb, h):
+        direct, _, partner, further = plan(nb)
         for j in direct:
             direct_copy(j, h, partner, relay_send.at[0, j // 2]).wait_recv()
             relay_copy(j, h, partner, relay_send.at[0, j // 2]).start()
             if further is not None:
                 direct_copy(j, h, further, relay_send.at[1, j // 2]).start()
-        rate_q = rates[:, 0:1]
-        rate_k = rates[:, 1:2]
-        q_full = q[:, cols].astype(F32)
-        k_full = k[:, cols].astype(F32)
-        gain_q = gq[:, cols]
-        gain_k = gk[:, cols]
-        qn = (q_full * rate_q * gain_q).astype(BF16)
-        kn = (k_full * rate_k * gain_k).astype(BF16)
-        val = v[:, cols]
-        grad = g[:, cols]
-        scores = [dot_nt(qn, kn)]
-        grad_probs = [dot_nt(grad, val)]
-        for j in relayed:
-            relay_copy(j, h, partner, relay_send.at[0, j // 2]).wait_recv()
-        for j in range(nb):
-            scores.append(dot_nt(qn, clean[j, 0, :, cols]))
-            grad_probs.append(dot_nt(grad, clean[j, 1, :, cols]))
-        top = functools.reduce(jnp.maximum, [jnp.max(s, axis=1, keepdims=True) for s in scores])
-        expo = [jnp.exp2((s - top) * power) for s in scores]
-        total = functools.reduce(jnp.add, [jnp.sum(e, axis=1, keepdims=True) for e in expo])
-        summed = dot_nn(expo[0].astype(BF16), val)
-        for j in range(nb):
-            summed = summed + dot_nn(expo[j + 1].astype(BF16), clean[j, 1, :, cols])
-        inverse = 1.0 / total
-        attention = summed * inverse
-        att_out[:, cols] = attention.astype(BF16)
-        delta = jnp.sum(grad.astype(F32) * attention, axis=1, keepdims=True)
-        probs = [e * inverse for e in expo]
-        grad_scores = [(p * (d - delta)).astype(BF16) for p, d in zip(probs, grad_probs)]
-        grad_qn = dot_nn(grad_scores[0], kn)
-        for j in range(nb):
-            grad_qn = grad_qn + dot_nn(grad_scores[j + 1], clean[j, 0, :, cols])
-        grad_qn = grad_qn * scaling
-        grad_kn = dot_tn(grad_scores[0], qn) * scaling
-        dv_out[:, cols] = dot_tn(probs[0].astype(BF16), grad).astype(BF16)
-        store_grads(cols, q_full, k_full, grad_qn, grad_kn)
+
+    def row_sum(terms):
+        return functools.reduce(jnp.add, [jnp.sum(t, axis=1, keepdims=True) for t in terms])
+
+    def row_max(terms):
+        return functools.reduce(jnp.maximum, [jnp.max(t, axis=1, keepdims=True) for t in terms])
+
+    def weigh(blocks, operands):
+        return functools.reduce(jnp.add, [dot_nn(b, o) for b, o in zip(blocks, operands)])
+
+    def own_heads(nb, hs):
+        _, relayed, partner, _ = plan(nb)
+        cols = [columns(h) for h in hs]
+        q_full = [q[:, c].astype(F32) for c in cols]
+        k_full = [k[:, c].astype(F32) for c in cols]
+        qn = [(x * rates[:, 0:1] * gq[:, c]).astype(BF16) for x, c in zip(q_full, cols)]
+        kn = [(x * rates[:, 1:2] * gk[:, c]).astype(BF16) for x, c in zip(k_full, cols)]
+        grad = [g[:, c] for c in cols]
+        scores = [[dot_nt(a, b)] for a, b in zip(qn, kn)]
+        grad_probs = [[dot_nt(a, v[:, c])] for a, c in zip(grad, cols)]
+        for h in hs:
+            for j in relayed:
+                relay_copy(j, h, partner, relay_send.at[0, j // 2]).wait_recv()
+        keys = [[b] + [clean[j, 0, :, c] for j in range(nb)] for b, c in zip(kn, cols)]
+        values = [[v[:, c]] + [clean[j, 1, :, c] for j in range(nb)] for c in cols]
+        for i in range(len(hs)):
+            scores[i] += [dot_nt(qn[i], key) for key in keys[i][1:]]
+            grad_probs[i] += [dot_nt(grad[i], val) for val in values[i][1:]]
+        top = [row_max(s) for s in scores]
+        expo = [[jnp.exp2((x - t) * power) for x in s] for s, t in zip(scores, top)]
+        inverse = [1.0 / row_sum(e) for e in expo]
+        summed = [weigh([x.astype(BF16) for x in e], val) for e, val in zip(expo, values)]
+        attention = [s * i for s, i in zip(summed, inverse)]
+        for c, a in zip(cols, attention):
+            att_out[:, c] = a.astype(BF16)
+        delta = [row_sum([x.astype(F32) * a]) for x, a in zip(grad, attention)]
+        probs = [[x * i for x in e] for e, i in zip(expo, inverse)]
+        grad_scores = [
+            [(p * (d - x)).astype(BF16) for p, d in zip(ps, ds)] for ps, ds, x in zip(probs, grad_probs, delta)
+        ]
+        grad_qn = [weigh(s, key) * scaling for s, key in zip(grad_scores, keys)]
+        store_blocks(cols, q_full, k_full, qn, grad, grad_qn, grad_scores, probs)
+
+    def store_blocks(cols, q_full, k_full, qn, grad, grad_qn, grad_scores, probs):
+        grad_kn = [dot_tn(s[0], a) * scaling for s, a in zip(grad_scores, qn)]
+        grad_v = [dot_tn(p[0].astype(BF16), x) for p, x in zip(probs, grad)]
+        for c, x in zip(cols, grad_v):
+            dv_out[:, c] = x.astype(BF16)
+        for args in zip(cols, q_full, k_full, grad_qn, grad_kn):
+            store_grads(*args)
 
     def merged(mine, theirs):
         top1, total1, dot1 = [mine[:, i : i + 1] for i in range(3)]
@@ -303,38 +318,45 @@
         delta = (dot1 * weight1 + dot2 * weight2) * inverse
         return top, inverse, delta, weight1 * inverse, total2 * weight2 * inverse
 
-    def first_pass(r, qn, grad, keys, values):
-        scores = [dot_nt(qn, key) for key in keys]
-        top = functools.reduce(jnp.maximum, [jnp.max(s, axis=1, keepdims=True) for s in scores])
-        expo = [jnp.exp2((s - top) * power) for s in scores]
-        total = functools.reduce(jnp.add, [jnp.sum(e, axis=1, keepdims=True) for e in expo])
-        summed = functools.reduce(jnp.add, [dot_nn(e.astype(BF16), val) for e, val in zip(expo, values)])
-        near_trip[r, :, 0:1] = top
-        near_trip[r, :, 1:2] = total
-        near_trip[r, :, 2:3] = jnp.sum(grad.astype(F32) * summed, axis=1, keepdims=True)
+    def first_pass(rs, qn, grad, keys, values):
+        scores = [[dot_nt(a, key) for key in ks] for a, ks in zip(qn, keys)]
+        top = [row_max(s) for s in scores]
+        expo = [[jnp.exp2((x - t) * power) for x in s] for s, t in zip(scores, top)]
+        total = [row_sum(e) for e in expo]
+        summed = [weigh([x.astype(BF16) for x in e], val) for e, val in zip(expo, values)]
+        for i, r in enumerate(rs):
+            near_trip[r, :, 0:1] = top[i]
+            near_trip[r, :, 1:2] = total[i]
+            near_trip[r, :, 2:3] = row_sum([grad[i].astype(F32) * summed[i]])
         return summed, total
 
-    def second_pass(qn, grad, keys, values, top, inverse, delta):
-        probs = [jnp.exp2((dot_nt(qn, key) - top) * power) * inverse for key in keys]
-        grad_scores = [(p * (dot_nt(grad, val) - delta)).astype(BF16) for p, val in zip(probs, values)]
-        grad_qn = functools.reduce(jnp.add, [dot_nn(s, key) for s, key in zip(grad_scores, keys)]) * scaling
-        return probs[0], grad_scores[0], grad_qn
-
-    def trade(target):
+    def second_pass(qn, grad, keys, values, merge):
+        scores = [[dot_nt(a, key) for key in ks] for a, ks in zip(qn, keys)]
+        grad_probs = [[dot_nt(a, val) for val in vs] for a, vs in zip(grad, values)]
+        probs = [[jnp.exp2((x - m[0]) * power) * m[1] for x in s] for s, m in zip(scores, merge)]
+        grad_scores = [
+            [(p * (d - m[2])).astype(BF16) for p, d in zip(ps, ds)] for ps, ds, m in zip(probs, grad_probs, merge)
+        ]
+        return probs, grad_scores, [weigh(s, key) * scaling for s, key in zip(grad_scores, keys)]
+
+    def trade(p, target):
         lane = lax.broadcasted_iota(jnp.int32, (length, DH), 1)
         packed = jnp.zeros((length, DH), F32)
-        for r in range(lent):
+        for r in range(batch):
             for i in range(3):
-                packed = jnp.where(lane == 3 * r + i, near_trip[r, :, i : i + 1], packed)
-        trip_out[...] = jnp.transpose(packed)[: trip_out.shape[0]]
-        trip_copy(target).start()
-
-    def traded(target):
-        trip_copy(target).wait_recv()
-        unpacked = jnp.transpose(trip_in[...])
-        for r in range(lent):
+                packed = jnp.where(lane == 3 * r + i, near_trip[p * batch + r, :, i : i + 1], packed)
+        trip_out[p] = jnp.transpose(packed)[: trip_out.shape[1]]
+        trip_copy(p, target).start()
+
+    def traded(p, target):
+        trip_copy(p, target).wait_recv()
+        unpacked = jnp.transpose(trip_in[p])
+        for r in range(batch):
             for i in range(3):
-                far_trip[r, :, i : i + 1] = unpacked[:, 3 * r + i : 3 * r + i + 1]
+                far_trip[p * batch + r, :, i : i + 1] = unpacked[:, 3 * r + i : 3 * r + i + 1]
+
+    def batch_of(p):
+        return [p * batch + r for r in range(batch)]
 
     def far_operands(r):
         cols = columns(kept + r)
@@ -354,76 +376,37 @@
         values = [v[:, cols]] + [clean[j, 1, :, cols] for j in range(2, nb)]
         return cols, q_full, k_full, qn, g[:, cols], keys, values
 
-    def help_first(nb, r):
-        frame_copy(far.at[r], far.at[r], far_send.at[0], far_recv.at[r], nb + 2).wait_recv()
-        _, _, _, _, qn, grad, keys, values = far_operands(r)
-        summed, total = first_pass(r, qn, grad, keys, values)
-        back_out[1, r] = (summed / total).astype(BF16)
-
-    def help_second(r):
-        cols, q_full, rate, gain, qn, grad, keys, values = far_operands(r)
-        top, inverse, delta, _, _ = merged(near_trip[r], far_trip[r])
-        _, _, grad_qn = second_pass(qn, grad, keys, values, top, inverse, delta)
-        back_out[0, r] = grad_qn.astype(BF16)
-        far_inner[...] += q_full * (grad_qn * gain)
-        far_sums[pl.ds(r, 1), :] = jnp.sum(grad_qn * q_full * rate, axis=0, keepdims=True)
-
-    def near_first(nb, r):
-        _, _, _, qn, grad, keys, values = near_operands(nb, r)
-        part[r] = first_pass(r, qn, grad, keys, values)[0]
-
-    def near_second(nb, r):
-        cols, q_full, k_full, qn, grad, keys, values = near_operands(nb, r)
-        top, inverse, delta, near, far = merged(near_trip[r], far_trip[r])
-        part[r] = part[r] * near
-        far_trip[r, :, 3:4] = far
-        probs, grad_scores, grad_qn = second_pass(qn, grad, keys, values, top, inverse, delta)
-        grad_kn = dot_tn(grad_scores, qn) * scaling
-        dv_out[:, cols] = dot_tn(probs.astype(BF16), grad).astype(BF16)
-        store_grads(cols, q_full, k_full, grad_qn, grad_kn)
-
-    for nb in range(frames):
-
-        @pl.when(frame == nb)
-        def _():
-            own = functools.partial(head_step, nb)
-            if nb % 2 == 1:
-                partner_copy(nb - 1).wait_recv()
-            if helps(nb):
-                first, middle = head_count * 3 // 10, head_count // 2
-                repeat(0, first, own)
-                if nb == 0:
-                    partner_copy(1).wait_recv()
-                row_copy(nb + 2).wait_recv()
-                far_rates[...] = jnp.transpose(row_in[...])
-                repeat(0, lent // 2, functools.partial(help_first, nb))
-                repeat(first, middle, own)
-                repeat(lent // 2, lent, functools.partial(help_first, nb))
-                trade(nb + 2)
-                send_own(nb, kept - 1, kept)
-                far_inner[...] = jnp.zeros_like(far_inner)
-                traded(nb + 2)
-                repeat(0, lent, help_second)
-                row_out[...] = as_rows(far_inner[...], jnp.zeros_like(far_inner))
-                row_copy(nb + 2).start()
-                repeat(0, lent, lambda r: back_copy(0, r, nb + 2).start())
-                repeat(middle, head_count, own)
-                for r in range(lent):
-                    cols = columns(kept + r)
-                    sums1[me1, 0:1, cols] += far_sums[r : r + 1, :]
-                stats_go(1, as_rows(inner_q[...], inner_k[...]))
-            elif helped(nb):
-                repeat(0, lent, functools.partial(near_first, nb))
-                trade(nb - 2)
-                repeat(0, kept - 1, own)
-                traded(nb - 2)
-                repeat(0, lent, functools.partial(near_second, nb))
-                repeat(kept - 1, kept, own)
-                row_copy(nb - 2).wait_recv()
-                stats_go(1, as_rows(inner_q[...], inner_k[...]) + row_in[...])
-            else:
-                repeat(0, head_count, own)
-                stats_go(1, as_rows(inner_q[...], inner_k[...]))
+    def help_first(nb, rs):
+        for r in rs:
+            frame_copy(far.at[r], far.at[r], far_send.at[0], far_recv.at[r], nb + 2).wait_recv()
+        _, _, _, _, qn, grad, keys, values = zip(*[far_operands(r) for r in rs])
+        summed, total = first_pass(rs, qn, grad, keys, values)
+        for i, r in enumerate(rs):
+            back_out[1, r] = (summed[i] / total[i]).astype(BF16)
+
+    def help_second(rs):
+        cols, q_full, rate, gain, qn, grad, keys, values = zip(*[far_operands(r) for r in rs])
+        merge = [merged(near_trip[r], far_trip[r]) for r in rs]
+        _, _, grad_qn = second_pass(qn, grad, keys, values, merge)
+        for i, r in enumerate(rs):
+            back_out[0, r] = grad_qn[i].astype(BF16)
+            far_inner[...] += q_full[i] * (grad_qn[i] * gain[i])
+            far_sums[r : r + 1, :] = jnp.sum(grad_qn[i] * q_full[i] * rate[i], axis=0, keepdims=True)
+
+    def near_first(nb, rs):
+        _, _, _, qn, grad, keys, values = zip(*[near_operands(nb, r) for r in rs])
+        summed, _ = first_pass(rs, qn, grad, keys, values)
+        for i, r in enumerate(rs):
+            part[r] = summed[i]
+
+    def near_second(nb, rs):
+        cols, q_full, k_full, qn, grad, keys, values = zip(*[near_operands(nb, r) for r in rs])
+        merge = [merged(near_trip[r], far_trip[r]) for r in rs]
+        probs, grad_scores, grad_qn = second_pass(qn, grad, keys, values, merge)
+        store_blocks(cols, q_full, k_full, qn, grad, grad_qn, grad_scores, probs)
+        for m, r in zip(merge, rs):
+            part[r] = part[r] * m[3]
+            far_trip[r, :, 3:4] = m[4]
 
     def s1_copy(d, part):
         return pltpu.make_async_remote_copy(
@@ -435,6 +418,79 @@
             device_id_type=MESH,
         )
 
+    def send_sums():
+        repeat(1, n1, lambda d: s1_copy(d, sums1.at[me1]).start())
+
+    def own_range(nb, first, last):
+        repeat(first // group, last // group, lambda i: own_heads(nb, [group * i + x for x in range(group)]))
+
+    for nb in range(frames):
+
+        @pl.when(frame == nb)
+        def _():
+            if nb % 2 == 1:
+                partner_copy(nb - 1).wait_recv()
+            if helps(nb):
+                other = nb + 2
+                first = head_count * 2 // 5 // group * group
+                middle = head_count * 3 // 5 // group * group
+                own_range(nb, 0, first)
+                if nb == 0:
+                    partner_copy(1).wait_recv()
+                row_copy(other).wait_recv()
+                far_rates[...] = jnp.transpose(row_in[...])
+                far_inner[...] = jnp.zeros_like(far_inner)
+                help_first(nb, batch_of(0))
+                trade(0, other)
+                send_own(nb, kept - 2, kept)
+                own_range(nb, first, middle)
+                traded(0, other)
+                help_second(batch_of(0))
+                help_first(nb, batch_of(1))
+                trade(1, other)
+                repeat(0, batch, lambda r: back_copy(0, r, other).start())
+                traded(1, other)
+                help_second(batch_of(1))
+                row_out[...] = as_rows(far_inner[...], jnp.zeros_like(far_inner))
+                row_copy(other).start()
+                repeat(batch, lent, lambda r: back_copy(0, r, other).start())
+                own_range(nb, middle, head_count)
+                for r in range(lent):
+                    sums1[me1, 0:1, columns(kept + r)] += far_sums[r : r + 1, :]
+                send_sums()
+                repeat(0, lent, lambda r: back_copy(1, r, other).start())
+                stats_go(1, as_rows(inner_q[...], inner_k[...]))
+            elif helped(nb):
+                other = nb - 2
+                for p in range(2):
+                    near_first(nb, batch_of(p))
+                    trade(p, other)
+
+                def step(h):
+                    pass_on(nb, h)
+
+                    @pl.when((h == kept // 2) | (h == kept - 1))
+                    def _():
+                        p = jnp.where(h == kept - 1, 1, 0)
+                        traded(p, other)
+                        near_second(nb, batch_of(p))
+
+                    own_heads(nb, [h])
+
+                repeat(0, kept, step)
+                send_sums()
+                row_copy(other).wait_recv()
+                stats_go(1, as_rows(inner_q[...], inner_k[...]) + row_in[...])
+            else:
+
+                def step(h):
+                    pass_on(nb, h)
+                    own_heads(nb, [h])
+
+                repeat(0, head_count, step)
+                send_sums()
+                stats_go(1, as_rows(inner_q[...], inner_k[...]))
+
     def s2_copy(d, part):
         return pltpu.make_async_remote_copy(
             src_ref=part,
@@ -447,14 +503,6 @@
 
     all_s1 = s1_copy(1, sums1.at[pl.ds(0, n1 - 1)])
     all_s2 = s2_copy(1, sums2.at[pl.ds(0, n2 - 1)])
-    repeat(1, n1, lambda d: s1_copy(d, sums1.at[me1]).start())
-    for nb in range(frames):
-        if helps(nb):
-
-            @pl.when(frame == nb)
-            def _():
-                repeat(0, lent, lambda r: back_copy(1, r, nb + 2).start())
-
     inners = jnp.transpose(stats_total(1))
     rate_q = rates[:, 0:1]
     rate_k = rates[:, 1:2]
@@ -523,7 +571,8 @@
                     kept_heads(j, relay_send.at[t, j // 2]).wait_send()
             if helps(nb) or helped(nb):
                 other = nb + 2 if helps(nb) else nb - 2
-                trip_copy(other).wait_send()
+                for p in range(2):
+                    trip_copy(p, other).wait_send()
                 row_copy(other).wait_send()
             if helps(nb):
                 frame_copy(back_out, back_in, back_send.at[0], grad_recv.at[0], nb + 2).wait_send()
@@ -556,10 +605,10 @@
     dma = pltpu.SemaphoreType.DMA
     chips = max(frames // 2 - 1, 1)
     kept = 4 * 2 * length * width + 2 * 4 * features
-    lent = head_count * 2 // 5 if frames == 4 else 0
+    lent = head_count // 5 * 2 if frames == 4 else 0
     held = max(lent, 1)
     kept_count = head_count - lent
-    trip_rows = -(-3 * held // 8) * 8
+    trip_rows = -(-3 * (held // 2) // 8) * 8 if lent else 8
     outs = pl.pallas_call(
         functools.partial(kernel, frames, fsdp, heads_axis, width, features, lent),
         out_shape=(block, block, block, block, gains, gains),
@@ -586,8 +635,8 @@
             pltpu.VMEM((2, held, length, DH), BF16),
             pltpu.VMEM((held, length, 8), F32),
             pltpu.VMEM((held, length, 8), F32),
-            pltpu.VMEM((trip_rows, length), F32),
-            pltpu.VMEM((trip_rows, length), F32),
+            pltpu.VMEM((2, trip_rows, length), F32),
+            pltpu.VMEM((2, trip_rows, length), F32),
             pltpu.VMEM((8, length), F32),
             pltpu.VMEM((8, length), F32),
             dma((4,)),
@@ -605,8 +654,8 @@
             dma((1,)),
             dma((1,)),
             dma((held,)),
-            dma((2,)),
-            dma((2,)),
+            dma((3,)),
+            dma((3,)),
         ],
         compiler_params=pltpu.CompilerParams(
             collective_id=0, has_side_effects=True, vmem_limit_bytes=VMEM_BYTES - kept - 4096

time: 40.7 us -> 37.8 us (0.929)
  Pallas kernels: 39.7 us -> 36.8 us
    pallas_call x1, Pallas kernels: 38.2 us -> 35.3 us  [on_device(): pl.pallas_call(functools.partial(kernel, frames, fsdp, heads_axis, width,...]
where the time goes in v3:
time: 37.8 us; the launch traced here: 37.7 us
  Pallas kernels  36.8 us (97%)
  between operations  0.82 us (2%)
    pallas_call x1, Pallas kernels, on_device(): pl.pallas_call(functools.partial(kernel, frames, fsdp, heads_axis, width,...  35.3 us
    pallas_call x1, Pallas kernels, on_device(): pl.pallas_call(write_out, out_shape=tuple((jax.ShapeDtypeStruct(out.shape...  1.54 us

profile of v3, /device:TPU:0, one launch (start us, length us, event | category | flops | bytes accessed | tf_op | source)
XLA Modules:
  0.0 37.7 jit_solution(11839554984188392284)
XLA Ops:
  0.6 35.3 %attention.1 = (bf16[256,1280]{1,0:T(8,128)(2,1)S(1)}, bf16[256,1280]{1,0:T(8,128)(2,1)S(1)}, bf16[256,1280]{1,0:T(8,128)(2,1)S(1)}, bf16[256,1280]{1,0:T(8,128)...) custom-call(bf16[256,1280]{1,0:T(8,128)(2,1)} %q_hbm.1, bf16[256,1280]{1,0:T(8,128)(2,1)} %k_hbm.1, ...), custom_call_target="tpu_custom_call" | custom-call | tf_op jit(solution)/shard_map/attention/pallas_call | solution.py:612
  35.9 1.5 %write_out.1 = (bf16[256,1280]{1,0:T(8,128)(2,1)}, bf16[256,1280]{1,0:T(8,128)(2,1)}, bf16[256,1280]{1,0:T(8,128)(2,1)}, bf16[256,1280]{1,0:T(8,128)(2,1)}, f32[1,5120]{1,0:T(1,128)}, /*index=5*/f32[1,5120]{1,0:T(1,128)}) custom-call(bf16[256,1280]{1,0:T(8,128)(2,1)S(1)} %get-tuple-element.18.refs_0_, bf16[256,1280]{1,0:T(8,128)(2,1)S(1)} %get-tuple-element.19.refs_1_, ...), custom_call_target="tpu_custom_call" | custom-call | tf_op jit(solution)/shard_map/write_out/pallas_call | solution.py:668

commit v4 on v3

--- a/solution.py
+++ b/solution.py
@@ -33,15 +33,16 @@
     q_hbm, k_hbm, v_hbm, ck_hbm, cv_hbm, gq_hbm, gk_hbm, g_hbm,
     att_out, dq_out, dk_out, dv_out, gain_q_out, gain_k_out,
     tokens, gains, clean, flat_q, flat_k, inner_q, inner_k, rates,
-    stats, sums1, sums2, far, far_rates, far_inner, far_sums, part, back_out, back_in,
+    stats, sums, sums1, sums2, ends, far_sum, far, far_rates, far_inner, far_sums, part, back_out, back_in,
     near_trip, far_trip, trip_out, trip_in, row_out, row_in,
     load_sem, own_send, relay_send, direct_recv, relay_recv, partner_recv, stats_send, stats_recv, sum_send, sum_recv,
-    far_send, far_recv, back_send, grad_recv, att_recv, row_send, row_recv,
+    far_send, far_recv, back_send, grad_recv, att_recv, row_send, row_recv, end_send, end_recv,
 ):
     q, k, v, g = [tokens.at[i] for i in range(4)]
     gq, gk = gains.at[0], gains.at[1]
     length = tokens.shape[1]
     head_count = width // DH
+    devices = frames * fsdp * heads_axis
     kept = head_count - lent
     batch = lent // 2
     group = 2 - head_count % 2
@@ -152,33 +153,36 @@
         further = plan(nb)[3]
         repeat(first, last, lambda h: direct_copy(nb, h, further, own_send.at[0]).start())
 
-    def far_copy(kind, r, target):
+    def far_copy(kind, r, p, target):
         src = (q_hbm, g_hbm)[kind].at[:, columns(kept + r)]
-        return frame_copy(src, far.at[r, kind], far_send.at[0], far_recv.at[r], target)
+        return frame_copy(src, far.at[r, kind], far_send.at[0], far_recv.at[p], target)
 
     def back_copy(kind, r, target):
         recv = grad_recv.at[0] if kind == 0 else att_recv.at[r]
         return frame_copy(back_out.at[kind, r], back_in.at[kind, r], back_send.at[0], recv, target)
 
     def trip_copy(p, target):
-        return frame_copy(trip_out.at[p], trip_in.at[p], row_send.at[1 + p], row_recv.at[1 + p], target)
+        return frame_copy(trip_out.at[p], trip_in.at[p], row_send.at[1], row_recv.at[1 + p], target)
+
+    def sum_copy(target):
+        return frame_copy(sums, far_sum, row_send.at[2], row_recv.at[3], target)
 
     def row_copy(target):
         return frame_copy(row_out, row_in, row_send.at[0], row_recv.at[0], target)
 
-    def lend(nb, first, last):
+    def lend(nb, p):
         def go(r):
             for kind in range(2):
-                far_copy(kind, r, nb - 2).start()
-
-        repeat(first, last, go)
+                far_copy(kind, r, p, nb - 2).start()
+
+        repeat(p * batch, (p + 1) * batch, go)
 
     for nb in range(frames):
 
         @pl.when(frame == nb)
         def _():
             if helped(nb):
-                lend(nb, 0, batch)
+                lend(nb, 0)
             if nb < frames - 1:
                 arrive(clean.at[nb], load_sem.at[3])
             if plan(nb)[3] is not None:
@@ -197,7 +201,7 @@
         return pltpu.make_async_remote_copy(
             src_ref=part,
             dst_ref=part,
-            send_sem=stats_send.at[phase],
+            send_sem=stats_send.at[0],
             recv_sem=stats_recv.at[phase],
             device_id=peer2(d),
             device_id_type=MESH,
@@ -236,9 +240,9 @@
 
             @pl.when(frame == nb)
             def _():
-                row_out[...] = rate_rows
+                row_out[...] = rate_rows[0:2]
                 row_copy(nb - 2).start()
-                lend(nb, batch, lent)
+                lend(nb, 1)
 
     def store_grads(cols, q_full, k_full, grad_qn, grad_kn):
         fq = grad_qn * gq[:, cols]
@@ -247,8 +251,8 @@
         flat_k[:, cols] = fk
         inner_q[...] += q_full * fq
         inner_k[...] += k_full * fk
-        sums1[me1, 0:1, cols] = jnp.sum(grad_qn * q_full * rates[:, 0:1], axis=0, keepdims=True)
-        sums1[me1, 1:2, cols] = jnp.sum(grad_kn * k_full * rates[:, 1:2], axis=0, keepdims=True)
+        sums[0:1, cols] = jnp.sum(grad_qn * q_full * rates[:, 0:1], axis=0, keepdims=True)
+        sums[1:2, cols] = jnp.sum(grad_kn * k_full * rates[:, 1:2], axis=0, keepdims=True)
 
     def pass_on(nb, h):
         direct, _, partner, further = plan(nb)
@@ -376,9 +380,10 @@
         values = [v[:, cols]] + [clean[j, 1, :, cols] for j in range(2, nb)]
         return cols, q_full, k_full, qn, g[:, cols], keys, values
 
-    def help_first(nb, rs):
-        for r in rs:
-            frame_copy(far.at[r], far.at[r], far_send.at[0], far_recv.at[r], nb + 2).wait_recv()
+    def help_first(nb, p):
+        rs = batch_of(p)
+        land = far.at[pl.ds(p * batch, batch)]
+        frame_copy(land, land, far_send.at[0], far_recv.at[p], nb + 2).wait_recv()
         _, _, _, _, qn, grad, keys, values = zip(*[far_operands(r) for r in rs])
         summed, total = first_pass(rs, qn, grad, keys, values)
         for i, r in enumerate(rs):
@@ -418,8 +423,29 @@
             device_id_type=MESH,
         )
 
-    def send_sums():
-        repeat(1, n1, lambda d: s1_copy(d, sums1.at[me1]).start())
+    slots = 2 * videos if lent else n1
+    high = me1 - n1 + slots
+
+    def send_sums(addend):
+        sums1[high] = sums[...] + addend
+        repeat(1, n1, lambda d: s1_copy(d, sums1.at[high]).start())
+
+    def end_copy(d, part):
+        p = lax.rem((frame * fsdp + fs) * heads_axis + lax.axis_index("head") + d, devices)
+        return pltpu.make_async_remote_copy(
+            src_ref=part,
+            dst_ref=part,
+            send_sem=end_send.at[0],
+            recv_sem=end_recv.at[0],
+            device_id={
+                "frame": p // (fsdp * heads_axis),
+                "fsdp": lax.rem(p // heads_axis, fsdp),
+                "head": lax.rem(p, heads_axis),
+            },
+            device_id_type=MESH,
+        )
+
+    last = pl.ds((kept - 1) * DH, DH)
 
     def own_range(nb, first, last):
         repeat(first // group, last // group, lambda i: own_heads(nb, [group * i + x for x in range(group)]))
@@ -433,31 +459,29 @@
             if helps(nb):
                 other = nb + 2
                 first = head_count * 2 // 5 // group * group
-                middle = head_count * 3 // 5 // group * group
                 own_range(nb, 0, first)
                 if nb == 0:
                     partner_copy(1).wait_recv()
                 row_copy(other).wait_recv()
-                far_rates[...] = jnp.transpose(row_in[...])
+                far_rates[:, 0:2] = jnp.transpose(row_in[...])
                 far_inner[...] = jnp.zeros_like(far_inner)
-                help_first(nb, batch_of(0))
+                help_first(nb, 0)
                 trade(0, other)
                 send_own(nb, kept - 2, kept)
-                own_range(nb, first, middle)
+                own_range(nb, first, head_count)
                 traded(0, other)
                 help_second(batch_of(0))
-                help_first(nb, batch_of(1))
+                help_first(nb, 1)
                 trade(1, other)
-                repeat(0, batch, lambda r: back_copy(0, r, other).start())
+                back_copy(0, 0, other).start()
                 traded(1, other)
                 help_second(batch_of(1))
-                row_out[...] = as_rows(far_inner[...], jnp.zeros_like(far_inner))
+                for r in range(lent):
+                    sums[0:1, columns(kept + r)] += far_sums[r : r + 1, :]
+                sum_copy(other).start()
+                row_out[...] = as_rows(far_inner[...], jnp.zeros_like(far_inner))[0:2]
                 row_copy(other).start()
-                repeat(batch, lent, lambda r: back_copy(0, r, other).start())
-                own_range(nb, middle, head_count)
-                for r in range(lent):
-                    sums1[me1, 0:1, columns(kept + r)] += far_sums[r : r + 1, :]
-                send_sums()
+                repeat(1, lent, lambda r: back_copy(0, r, other).start())
                 repeat(0, lent, lambda r: back_copy(1, r, other).start())
                 stats_go(1, as_rows(inner_q[...], inner_k[...]))
             elif helped(nb):
@@ -466,6 +490,8 @@
                     near_first(nb, batch_of(p))
                     trade(p, other)
 
+                sums[:, last] = jnp.zeros((2, DH), F32)
+
                 def step(h):
                     pass_on(nb, h)
 
@@ -475,12 +501,20 @@
                         traded(p, other)
                         near_second(nb, batch_of(p))
 
+                    @pl.when(h == kept - 1)
+                    def _():
+                        sum_copy(other).wait_recv()
+                        send_sums(far_sum[...])
+
                     own_heads(nb, [h])
 
                 repeat(0, kept, step)
-                send_sums()
                 row_copy(other).wait_recv()
-                stats_go(1, as_rows(inner_q[...], inner_k[...]) + row_in[...])
+                rows = as_rows(inner_q[...], inner_k[...])
+                stats_go(1, jnp.where(row == 0, rows + row_in[0:1], rows))
+                end = me2 * slots + high
+                ends[end] = sums[:, last]
+                repeat(1, devices, lambda d: end_copy(d, ends.at[end]).start())
             else:
 
                 def step(h):
@@ -488,7 +522,7 @@
                     own_heads(nb, [h])
 
                 repeat(0, head_count, step)
-                send_sums()
+                send_sums(0.0)
                 stats_go(1, as_rows(inner_q[...], inner_k[...]))
 
     def s2_copy(d, part):
@@ -501,19 +535,26 @@
             device_id_type=MESH,
         )
 
-    all_s1 = s1_copy(1, sums1.at[pl.ds(0, n1 - 1)])
+    def only(which, action):
+        for nb in range(frames):
+            if which(nb):
+                pl.when(frame == nb)(action)
+
     all_s2 = s2_copy(1, sums2.at[pl.ds(0, n2 - 1)])
+    if lent:
+        only(helps, s1_copy(1, sums1.at[pl.ds(0, slots)]).wait_recv)
+        only(helped, s1_copy(1, sums1.at[pl.ds(0, slots - 1)]).wait_recv)
+    else:
+        s1_copy(1, sums1.at[pl.ds(0, slots - 1)]).wait_recv()
+    sums2[me2] = jnp.sum(sums1[pl.ds(0, slots)], axis=0)
+    for d in range(1, n2):
+        s2_copy(d, sums2.at[me2]).start()
     inners = jnp.transpose(stats_total(1))
     rate_q = rates[:, 0:1]
     rate_k = rates[:, 1:2]
     cube_q = rate_q * rate_q * rate_q * inners[:, 0:1] / features
     cube_k = rate_k * rate_k * rate_k * inners[:, 1:2] / features
 
-    all_s1.wait_recv()
-    sums2[me2] = jnp.sum(sums1[...], axis=0)
-    for d in range(1, n2):
-        s2_copy(d, sums2.at[me2]).start()
-
     def finish(h, _):
         cols = columns(h)
         dq_out[:, cols] = (rate_q * flat_q[:, cols] - q[:, cols].astype(F32) * cube_q).astype(BF16)
@@ -540,6 +581,14 @@
     for p in range(n2):
         gain_q_out[:, p * width : (p + 1) * width] = sums2[p, 0:1, :]
         gain_k_out[:, p * width : (p + 1) * width] = sums2[p, 1:2, :]
+    if lent:
+        only(helps, end_copy(1, ends.at[pl.ds(0, n2 * slots)]).wait_recv)
+        only(helped, end_copy(1, ends.at[pl.ds(0, n2 * slots - 1)]).wait_recv)
+        for p in range(n2):
+            late = jnp.sum(ends[pl.ds(p * slots, slots)], axis=0)
+            cols = pl.ds(p * width + (kept - 1) * DH, DH)
+            gain_q_out[:, cols] += late[0:1]
+            gain_k_out[:, cols] += late[1:2]
 
     for nb in range(frames):
         if helped(nb):
@@ -553,9 +602,13 @@
 
                 repeat(0, lent, join)
 
-    all_stats(0).wait_send()
-    all_stats(1).wait_send()
-    all_s1.wait_send()
+    stats_copy(0, 1, stats.at[:, pl.ds(0, n2 - 1)]).wait_send()
+    if lent:
+        only(helped, s1_copy(1, sums1.at[pl.ds(0, n1 - 1)]).wait_send)
+        only(helped, end_copy(1, ends.at[pl.ds(0, devices - 1)]).wait_send)
+        only(helps, lambda: sum_copy(2).wait_send())
+    else:
+        s1_copy(1, sums1.at[pl.ds(0, n1 - 1)]).wait_send()
     all_s2.wait_send()
     for nb in range(frames):
         direct, _, _, further = plan(nb)
@@ -571,8 +624,7 @@
                     kept_heads(j, relay_send.at[t, j // 2]).wait_send()
             if helps(nb) or helped(nb):
                 other = nb + 2 if helps(nb) else nb - 2
-                for p in range(2):
-                    trip_copy(p, other).wait_send()
+                frame_copy(trip_out, trip_in, row_send.at[1], row_recv.at[1], other).wait_send()
                 row_copy(other).wait_send()
             if helps(nb):
                 frame_copy(back_out, back_in, back_send.at[0], grad_recv.at[0], nb + 2).wait_send()
@@ -624,8 +676,11 @@
             pltpu.VMEM((length, DH), F32),
             pltpu.VMEM((length, 8), F32),
             pltpu.VMEM((2, n2, 8, length), F32),
+            pltpu.VMEM((2, width), F32),
             pltpu.VMEM((n1, 2, width), F32),
             pltpu.VMEM((n2, 2, width), F32),
+            pltpu.VMEM((frames * fsdp * heads_axis if lent else 1, 2, DH), F32),
+            pltpu.VMEM((2, width), F32),
             pltpu.VMEM((held, 2, length, DH), BF16),
             pltpu.VMEM((length, 8), F32),
             pltpu.VMEM((length, DH), F32),
@@ -637,25 +692,27 @@
             pltpu.VMEM((held, length, 8), F32),
             pltpu.VMEM((2, trip_rows, length), F32),
             pltpu.VMEM((2, trip_rows, length), F32),
-            pltpu.VMEM((8, length), F32),
-            pltpu.VMEM((8, length), F32),
+            pltpu.VMEM((2, length), F32),
+            pltpu.VMEM((2, length), F32),
             dma((4,)),
             dma((2,)),
-            dma((2, chips)),
+            dma((min(chips, 2), chips)),
             dma((chips, kept_count)),
             dma((chips, kept_count)),
+            dma((1,)),
             dma((1,)),
             dma((2,)),
             dma((2,)),
             dma((2,)),
+            dma((1,)),
             dma((2,)),
-            dma((1,)),
-            dma((held,)),
             dma((1,)),
             dma((1,)),
             dma((held,)),
             dma((3,)),
-            dma((3,)),
+            dma((4,)),
+            dma((1,)),
+            dma((1,)),
         ],
         compiler_params=pltpu.CompilerParams(
             collective_id=0, has_side_effects=True, vmem_limit_bytes=VMEM_BYTES - kept - 4096

time: 37.8 us -> 36.8 us (0.974)
  Pallas kernels: 36.8 us -> 35.9 us
    pallas_call x1, Pallas kernels: 35.3 us -> 34.3 us  [on_device(): pl.pallas_call(functools.partial(kernel, frames, fsdp, heads_axis, width,...]
where the time goes in v4:
time: 36.8 us; the launch traced here: 36.7 us
  Pallas kernels  35.9 us (98%)
  between operations  0.82 us (2%)
    pallas_call x1, Pallas kernels, on_device(): pl.pallas_call(functools.partial(kernel, frames, fsdp, heads_axis, width,...  34.3 us
    pallas_call x1, Pallas kernels, on_device(): pl.pallas_call(write_out, out_shape=tuple((jax.ShapeDtypeStruct(out.shape...  1.54 us

profile of v4, /device:TPU:0, one launch (start us, length us, event | category | flops | bytes accessed | tf_op | source)
XLA Modules:
  0.0 36.7 jit_solution(1148170867606230153)
XLA Ops:
  0.6 34.3 %attention.1 = (bf16[256,1280]{1,0:T(8,128)(2,1)S(1)}, bf16[256,1280]{1,0:T(8,128)(2,1)S(1)}, bf16[256,1280]{1,0:T(8,128)(2,1)S(1)}, bf16[256,1280]{1,0:T(8,128)...) custom-call(bf16[256,1280]{1,0:T(8,128)(2,1)} %q_hbm.1, bf16[256,1280]{1,0:T(8,128)(2,1)} %k_hbm.1, ...), custom_call_target="tpu_custom_call" | custom-call | tf_op jit(solution)/shard_map/attention/pallas_call | solution.py:664
  35.0 1.5 %write_out.1 = (bf16[256,1280]{1,0:T(8,128)(2,1)}, bf16[256,1280]{1,0:T(8,128)(2,1)}, bf16[256,1280]{1,0:T(8,128)(2,1)}, bf16[256,1280]{1,0:T(8,128)(2,1)}, f32[1,5120]{1,0:T(1,128)}, /*index=5*/f32[1,5120]{1,0:T(1,128)}) custom-call(bf16[256,1280]{1,0:T(8,128)(2,1)S(1)} %get-tuple-element.18.refs_0_, bf16[256,1280]{1,0:T(8,128)(2,1)S(1)} %get-tuple-element.19.refs_1_, ...), custom_call_target="tpu_custom_call" | custom-call | tf_op jit(solution)/shard_map/write_out/pallas_call | solution.py:725

commit v5 on v4

--- a/solution.py
+++ b/solution.py
@@ -32,11 +32,11 @@
     frames, fsdp, heads_axis, width, features, lent,
     q_hbm, k_hbm, v_hbm, ck_hbm, cv_hbm, gq_hbm, gk_hbm, g_hbm,
     att_out, dq_out, dk_out, dv_out, gain_q_out, gain_k_out,
-    tokens, gains, clean, flat_q, flat_k, inner_q, inner_k, rates,
-    stats, sums, sums1, sums2, ends, far_sum, far, far_rates, far_inner, far_sums, part, back_out, back_in,
+    tokens, gains, clean, flat_q, flat_k, inner_q, inner_k, wide,
+    stats, sums, sums1, sums2, ends, far_sum, far, far_wide, far_inner, far_sums, part, back_out, back_in,
     near_trip, far_trip, trip_out, trip_in, row_out, row_in,
     load_sem, own_send, relay_send, direct_recv, relay_recv, partner_recv, stats_send, stats_recv, sum_send, sum_recv,
-    far_send, far_recv, back_send, grad_recv, att_recv, row_send, row_recv, end_send, end_recv,
+    far_send, far_recv, back_send, grad_recv, att_recv, row_send, row_recv, end_send, end_recv, ready,
 ):
     q, k, v, g = [tokens.at[i] for i in range(4)]
     gq, gk = gains.at[0], gains.at[1]
@@ -44,7 +44,8 @@
     head_count = width // DH
     devices = frames * fsdp * heads_axis
     kept = head_count - lent
-    batch = lent // 2
+    batches = [list(range(1, lent)), [0]]
+    order = batches[0] + batches[1]
     group = 2 - head_count % 2
     videos = fsdp // 2
     scaling = 1.0 / math.sqrt(DH)
@@ -88,13 +89,25 @@
 
     barrier = pltpu.get_barrier_semaphore()
 
-    def greet(d, _):
-        pl.semaphore_signal(barrier, inc=1, device_id=peer1(d), device_id_type=MESH)
-        return 0
-
-    lax.fori_loop(1, n1, greet, 0)
-    for d in range(1, n2):
-        pl.semaphore_signal(barrier, inc=1, device_id=peer2(d), device_id_type=MESH)
+    groups = videos - 1 + n2 - 1
+    if lent:
+        mates = [{"frame": jnp.int32(f)} for f in range(frames)]
+        for f in range(frames):
+
+            @pl.when(frame != f)
+            def _():
+                pl.semaphore_signal(barrier, inc=1, device_id=mates[f], device_id_type=MESH)
+
+        for f in range(1, frames, 2):
+            for d in range(1, videos):
+                near = {"fsdp": half * videos + lax.rem(video + d, videos)}
+                pl.semaphore_signal(barrier, inc=1, device_id={**near, **mates[f]}, device_id_type=MESH)
+            for d in range(1, n2):
+                pl.semaphore_signal(barrier, inc=1, device_id={**peer2(d), **mates[f]}, device_id_type=MESH)
+    else:
+        repeat(1, n1, lambda d: pl.semaphore_signal(barrier, inc=1, device_id=peer1(d), device_id_type=MESH))
+        for d in range(1, n2):
+            pl.semaphore_signal(barrier, inc=1, device_id=peer2(d), device_id_type=MESH)
     start = pl.multiple_of(me2 * width, DH)
     for src, dst, i in (
         (q_hbm, q, 0),
@@ -105,7 +118,15 @@
         (g_hbm, g, 2),
     ):
         pltpu.make_async_copy(src, dst, load_sem.at[i]).start()
-    pl.semaphore_wait(barrier, n1 - 1 + n2 - 1)
+    if lent:
+        pl.semaphore_wait(barrier, frames - 1 + lax.rem(frame, 2) * (frames * groups))
+
+        @pl.when(lax.rem(frame, 2) == 1)
+        def _():
+            pl.semaphore_signal(ready, inc=1, device_id={"frame": frame - 1}, device_id_type=MESH)
+
+    else:
+        pl.semaphore_wait(barrier, n1 - 1 + n2 - 1)
 
     def frame_copy(src, dst, send, recv, target):
         return pltpu.make_async_remote_copy(
@@ -153,16 +174,17 @@
         further = plan(nb)[3]
         repeat(first, last, lambda h: direct_copy(nb, h, further, own_send.at[0]).start())
 
-    def far_copy(kind, r, p, target):
+    def far_copy(kind, r, target):
         src = (q_hbm, g_hbm)[kind].at[:, columns(kept + r)]
-        return frame_copy(src, far.at[r, kind], far_send.at[0], far_recv.at[p], target)
+        return frame_copy(src, far.at[r, kind], far_send.at[0], far_recv.at[0 if r in batches[0] else 1], target)
 
     def back_copy(kind, r, target):
         recv = grad_recv.at[0] if kind == 0 else att_recv.at[r]
         return frame_copy(back_out.at[kind, r], back_in.at[kind, r], back_send.at[0], recv, target)
 
     def trip_copy(p, target):
-        return frame_copy(trip_out.at[p], trip_in.at[p], row_send.at[1], row_recv.at[1 + p], target)
+        rs = pl.ds(batches[p][0], len(batches[p]))
+        return frame_copy(trip_out.at[rs], trip_in.at[rs], row_send.at[1], row_recv.at[1 + p], target)
 
     def sum_copy(target):
         return frame_copy(sums, far_sum, row_send.at[2], row_recv.at[3], target)
@@ -170,23 +192,21 @@
     def row_copy(target):
         return frame_copy(row_out, row_in, row_send.at[0], row_recv.at[0], target)
 
-    def lend(nb, p):
-        def go(r):
+    def lend(nb, first, last):
+        for r in order[first:last]:
             for kind in range(2):
-                far_copy(kind, r, p, nb - 2).start()
-
-        repeat(p * batch, (p + 1) * batch, go)
+                far_copy(kind, r, nb - 2).start()
 
     for nb in range(frames):
 
         @pl.when(frame == nb)
         def _():
             if helped(nb):
-                lend(nb, 0)
+                lend(nb, 0, lent // 2)
             if nb < frames - 1:
                 arrive(clean.at[nb], load_sem.at[3])
             if plan(nb)[3] is not None:
-                send_own(nb, 0, kept - 2 if helps(nb) else kept)
+                send_own(nb, 0, kept - 1 if helps(nb) else kept)
             if has_partner_copy(nb):
                 partner_copy(nb).start()
 
@@ -228,13 +248,21 @@
             total = total + x * x
         return total
 
+    if lent:
+
+        @pl.when(lax.rem(frame, 2) == 0)
+        def _():
+            pl.semaphore_wait(ready, 1)
+
     stats_go(0, as_rows(square(q), square(k)))
     inner_q[...] = jnp.zeros_like(inner_q)
     inner_k[...] = jnp.zeros_like(inner_k)
     arrive(gains, load_sem.at[1])
     arrive(tokens.at[pl.ds(2, 2)], load_sem.at[2])
     rate_rows = lax.rsqrt(stats_total(0) / features + EPSILON)
-    rates[...] = jnp.transpose(rate_rows)
+    rate_columns = jnp.transpose(rate_rows)
+    for i in range(2):
+        wide[i] = jnp.broadcast_to(rate_columns[:, i : i + 1], (length, DH))
     for nb in range(frames):
         if helped(nb):
 
@@ -242,7 +270,7 @@
             def _():
                 row_out[...] = rate_rows[0:2]
                 row_copy(nb - 2).start()
-                lend(nb, 1)
+                lend(nb, lent // 2, lent)
 
     def store_grads(cols, q_full, k_full, grad_qn, grad_kn):
         fq = grad_qn * gq[:, cols]
@@ -251,8 +279,8 @@
         flat_k[:, cols] = fk
         inner_q[...] += q_full * fq
         inner_k[...] += k_full * fk
-        sums[0:1, cols] = jnp.sum(grad_qn * q_full * rates[:, 0:1], axis=0, keepdims=True)
-        sums[1:2, cols] = jnp.sum(grad_kn * k_full * rates[:, 1:2], axis=0, keepdims=True)
+        sums[0:1, cols] = jnp.sum(grad_qn * q_full * wide[0], axis=0, keepdims=True)
+        sums[1:2, cols] = jnp.sum(grad_kn * k_full * wide[1], axis=0, keepdims=True)
 
     def pass_on(nb, h):
         direct, _, partner, further = plan(nb)
@@ -276,8 +304,8 @@
         cols = [columns(h) for h in hs]
         q_full = [q[:, c].astype(F32) for c in cols]
         k_full = [k[:, c].astype(F32) for c in cols]
-        qn = [(x * rates[:, 0:1] * gq[:, c]).astype(BF16) for x, c in zip(q_full, cols)]
-        kn = [(x * rates[:, 1:2] * gk[:, c]).astype(BF16) for x, c in zip(k_full, cols)]
+        qn = [(x * wide[0] * gq[:, c]).astype(BF16) for x, c in zip(q_full, cols)]
+        kn = [(x * wide[1] * gk[:, c]).astype(BF16) for x, c in zip(k_full, cols)]
         grad = [g[:, c] for c in cols]
         scores = [[dot_nt(a, b)] for a, b in zip(qn, kn)]
         grad_probs = [[dot_nt(a, v[:, c])] for a, c in zip(grad, cols)]
@@ -346,26 +374,23 @@
     def trade(p, target):
         lane = lax.broadcasted_iota(jnp.int32, (length, DH), 1)
         packed = jnp.zeros((length, DH), F32)
-        for r in range(batch):
+        for x, r in enumerate(batches[p]):
             for i in range(3):
-                packed = jnp.where(lane == 3 * r + i, near_trip[p * batch + r, :, i : i + 1], packed)
-        trip_out[p] = jnp.transpose(packed)[: trip_out.shape[1]]
+                packed = jnp.where(lane == 4 * x + i, near_trip[r, :, i : i + 1], packed)
+        rows = jnp.transpose(packed)
+        for x, r in enumerate(batches[p]):
+            trip_out[r] = rows[4 * x : 4 * x + 4]
         trip_copy(p, target).start()
 
     def traded(p, target):
         trip_copy(p, target).wait_recv()
-        unpacked = jnp.transpose(trip_in[p])
-        for r in range(batch):
-            for i in range(3):
-                far_trip[p * batch + r, :, i : i + 1] = unpacked[:, 3 * r + i : 3 * r + i + 1]
-
-    def batch_of(p):
-        return [p * batch + r for r in range(batch)]
+        for r in batches[p]:
+            far_trip[r, :, 0:4] = jnp.transpose(trip_in[r])
 
     def far_operands(r):
         cols = columns(kept + r)
         q_full = far[r, 0].astype(F32)
-        rate, gain = far_rates[:, 0:1], gq[:, cols]
+        rate, gain = far_wide[...], gq[:, cols]
         keys = [clean[j, 0, :, cols] for j in range(2)]
         values = [clean[j, 1, :, cols] for j in range(2)]
         return cols, q_full, rate, gain, (q_full * rate * gain).astype(BF16), far[r, 1], keys, values
@@ -374,15 +399,15 @@
         cols = columns(kept + r)
         q_full = q[:, cols].astype(F32)
         k_full = k[:, cols].astype(F32)
-        qn = (q_full * rates[:, 0:1] * gq[:, cols]).astype(BF16)
-        kn = (k_full * rates[:, 1:2] * gk[:, cols]).astype(BF16)
+        qn = (q_full * wide[0] * gq[:, cols]).astype(BF16)
+        kn = (k_full * wide[1] * gk[:, cols]).astype(BF16)
         keys = [kn] + [clean[j, 0, :, cols] for j in range(2, nb)]
         values = [v[:, cols]] + [clean[j, 1, :, cols] for j in range(2, nb)]
         return cols, q_full, k_full, qn, g[:, cols], keys, values
 
     def help_first(nb, p):
-        rs = batch_of(p)
-        land = far.at[pl.ds(p * batch, batch)]
+        rs = batches[p]
+        land = far.at[pl.ds(rs[0], len(rs))]
         frame_copy(land, land, far_send.at[0], far_recv.at[p], nb + 2).wait_recv()
         _, _, _, _, qn, grad, keys, values = zip(*[far_operands(r) for r in rs])
         summed, total = first_pass(rs, qn, grad, keys, values)
@@ -445,7 +470,7 @@
             device_id_type=MESH,
         )
 
-    last = pl.ds((kept - 1) * DH, DH)
+    last = pl.ds((kept - 1) * DH, 2 * DH)
 
     def own_range(nb, first, last):
         repeat(first // group, last // group, lambda i: own_heads(nb, [group * i + x for x in range(group)]))
@@ -458,48 +483,46 @@
                 partner_copy(nb - 1).wait_recv()
             if helps(nb):
                 other = nb + 2
-                first = head_count * 2 // 5 // group * group
-                own_range(nb, 0, first)
+                own_range(nb, 0, head_count)
                 if nb == 0:
                     partner_copy(1).wait_recv()
                 row_copy(other).wait_recv()
-                far_rates[:, 0:2] = jnp.transpose(row_in[...])
+                far_wide[...] = jnp.broadcast_to(jnp.transpose(row_in[...])[:, 0:1], (length, DH))
                 far_inner[...] = jnp.zeros_like(far_inner)
                 help_first(nb, 0)
                 trade(0, other)
-                send_own(nb, kept - 2, kept)
-                own_range(nb, first, head_count)
+                send_own(nb, kept - 1, kept)
                 traded(0, other)
-                help_second(batch_of(0))
+                help_second(batches[0])
+                back_copy(0, order[0], other).start()
                 help_first(nb, 1)
                 trade(1, other)
-                back_copy(0, 0, other).start()
                 traded(1, other)
-                help_second(batch_of(1))
+                help_second(batches[1])
                 for r in range(lent):
                     sums[0:1, columns(kept + r)] += far_sums[r : r + 1, :]
                 sum_copy(other).start()
                 row_out[...] = as_rows(far_inner[...], jnp.zeros_like(far_inner))[0:2]
                 row_copy(other).start()
-                repeat(1, lent, lambda r: back_copy(0, r, other).start())
+                for r in order[1:]:
+                    back_copy(0, r, other).start()
                 repeat(0, lent, lambda r: back_copy(1, r, other).start())
                 stats_go(1, as_rows(inner_q[...], inner_k[...]))
             elif helped(nb):
                 other = nb - 2
                 for p in range(2):
-                    near_first(nb, batch_of(p))
+                    near_first(nb, batches[p])
                     trade(p, other)
 
-                sums[:, last] = jnp.zeros((2, DH), F32)
+                sums[:, last] = jnp.zeros((2, 2 * DH), F32)
 
                 def step(h):
                     pass_on(nb, h)
 
-                    @pl.when((h == kept // 2) | (h == kept - 1))
+                    @pl.when(h == kept - 2)
                     def _():
-                        p = jnp.where(h == kept - 1, 1, 0)
-                        traded(p, other)
-                        near_second(nb, batch_of(p))
+                        traded(0, other)
+                        near_second(nb, batches[0])
 
                     @pl.when(h == kept - 1)
                     def _():
@@ -509,6 +532,8 @@
                     own_heads(nb, [h])
 
                 repeat(0, kept, step)
+                traded(1, other)
+                near_second(nb, batches[1])
                 row_copy(other).wait_recv()
                 rows = as_rows(inner_q[...], inner_k[...])
                 stats_go(1, jnp.where(row == 0, rows + row_in[0:1], rows))
@@ -541,42 +566,55 @@
                 pl.when(frame == nb)(action)
 
     all_s2 = s2_copy(1, sums2.at[pl.ds(0, n2 - 1)])
+
+    def finish_heads():
+        inners = jnp.transpose(stats_total(1))
+        for i, inner in enumerate((inner_q, inner_k)):
+            full = jnp.broadcast_to(inners[:, i : i + 1], (length, DH))
+            inner[...] = wide[i] * wide[i] * wide[i] * full / features
+
+        def finish(h):
+            cols = columns(h)
+            dq_out[:, cols] = (wide[0] * flat_q[:, cols] - q[:, cols].astype(F32) * inner_q[...]).astype(BF16)
+            dk_out[:, cols] = (wide[1] * flat_k[:, cols] - k[:, cols].astype(F32) * inner_k[...]).astype(BF16)
+
+        repeat(0, head_count, finish)
+
+    def gather_sums(count):
+        s1_copy(1, sums1.at[pl.ds(0, count)]).wait_recv()
+        sums2[me2] = jnp.sum(sums1[pl.ds(0, slots)], axis=0)
+        for d in range(1, n2):
+            s2_copy(d, sums2.at[me2]).start()
+
     if lent:
-        only(helps, s1_copy(1, sums1.at[pl.ds(0, slots)]).wait_recv)
-        only(helped, s1_copy(1, sums1.at[pl.ds(0, slots - 1)]).wait_recv)
+
+        @pl.when(frame < 2)
+        def _():
+            finish_heads()
+            gather_sums(slots)
+
+        @pl.when(frame >= 2)
+        def _():
+            gather_sums(slots - 1)
+            grads = back_in.at[0]
+            frame_copy(grads, grads, back_send.at[0], grad_recv.at[0], 0).wait_recv()
+
+            def add(r):
+                cols = columns(kept + r)
+                flat_q[:, cols] += back_in[0, r].astype(F32) * gq[:, cols]
+
+            repeat(0, lent, add)
+            finish_heads()
+
     else:
-        s1_copy(1, sums1.at[pl.ds(0, slots - 1)]).wait_recv()
-    sums2[me2] = jnp.sum(sums1[pl.ds(0, slots)], axis=0)
-    for d in range(1, n2):
-        s2_copy(d, sums2.at[me2]).start()
-    inners = jnp.transpose(stats_total(1))
-    rate_q = rates[:, 0:1]
-    rate_k = rates[:, 1:2]
-    cube_q = rate_q * rate_q * rate_q * inners[:, 0:1] / features
-    cube_k = rate_k * rate_k * rate_k * inners[:, 1:2] / features
-
-    def finish(h, _):
-        cols = columns(h)
-        dq_out[:, cols] = (rate_q * flat_q[:, cols] - q[:, cols].astype(F32) * cube_q).astype(BF16)
-        dk_out[:, cols] = (rate_k * flat_k[:, cols] - k[:, cols].astype(F32) * cube_k).astype(BF16)
-        return 0
-
-    lax.fori_loop(0, kept, finish, 0)
-    for nb in range(frames):
-        if helped(nb):
-
-            @pl.when(frame == nb)
-            def _():
-                grads = back_in.at[0]
-                frame_copy(grads, grads, back_send.at[0], grad_recv.at[0], nb - 2).wait_recv()
-
-                def add(r):
-                    cols = columns(kept + r)
-                    flat_q[:, cols] += back_in[0, r].astype(F32) * gq[:, cols]
-
-                repeat(0, lent, add)
-
-    lax.fori_loop(kept, head_count, finish, 0)
+        gather_sums(slots - 1)
+        finish_heads()
+
+    def only(which, action):
+        for nb in range(frames):
+            if which(nb):
+                pl.when(frame == nb)(action)
+
     all_s2.wait_recv()
     for p in range(n2):
         gain_q_out[:, p * width : (p + 1) * width] = sums2[p, 0:1, :]
@@ -586,7 +624,7 @@
         only(helped, end_copy(1, ends.at[pl.ds(0, n2 * slots - 1)]).wait_recv)
         for p in range(n2):
             late = jnp.sum(ends[pl.ds(p * slots, slots)], axis=0)
-            cols = pl.ds(p * width + (kept - 1) * DH, DH)
+            cols = pl.ds(p * width + (kept - 1) * DH, 2 * DH)
             gain_q_out[:, cols] += late[0:1]
             gain_k_out[:, cols] += late[1:2]
 
@@ -657,10 +695,9 @@
     dma = pltpu.SemaphoreType.DMA
     chips = max(frames // 2 - 1, 1)
     kept = 4 * 2 * length * width + 2 * 4 * features
-    lent = head_count // 5 * 2 if frames == 4 else 0
+    lent = head_count // 5 * 2 if frames == 4 and head_count >= 5 else 0
     held = max(lent, 1)
     kept_count = head_count - lent
-    trip_rows = -(-3 * (held // 2) // 8) * 8 if lent else 8
     outs = pl.pallas_call(
         functools.partial(kernel, frames, fsdp, heads_axis, width, features, lent),
         out_shape=(block, block, block, block, gains, gains),
@@ -674,15 +711,15 @@
             pltpu.VMEM((length, width), F32),
             pltpu.VMEM((length, DH), F32),
             pltpu.VMEM((length, DH), F32),
-            pltpu.VMEM((length, 8), F32),
+            pltpu.VMEM((2, length, DH), F32),
             pltpu.VMEM((2, n2, 8, length), F32),
             pltpu.VMEM((2, width), F32),
             pltpu.VMEM((n1, 2, width), F32),
             pltpu.VMEM((n2, 2, width), F32),
-            pltpu.VMEM((frames * fsdp * heads_axis if lent else 1, 2, DH), F32),
+            pltpu.VMEM((frames * fsdp * heads_axis if lent else 1, 2, 2 * DH), F32),
             pltpu.VMEM((2, width), F32),
             pltpu.VMEM((held, 2, length, DH), BF16),
-            pltpu.VMEM((length, 8), F32),
+            pltpu.VMEM((length, DH), F32),
             pltpu.VMEM((length, DH), F32),
             pltpu.VMEM((-(-held // 8) * 8, DH), F32),
             pltpu.VMEM((held, length, DH), F32),
@@ -690,8 +727,8 @@
             pltpu.VMEM((2, held, length, DH), BF16),
             pltpu.VMEM((held, length, 8), F32),
             pltpu.VMEM((held, length, 8), F32),
-            pltpu.VMEM((2, trip_rows, length), F32),
-            pltpu.VMEM((2, trip_rows, length), F32),
+            pltpu.VMEM((held, 4, length), F32),
+            pltpu.VMEM((held, 4, length), F32),
             pltpu.VMEM((2, length), F32),
             pltpu.VMEM((2, length), F32),
             dma((4,)),
@@ -713,6 +750,7 @@
             dma((4,)),
             dma((1,)),
             dma((1,)),
+            pltpu.SemaphoreType.REGULAR,
         ],
         compiler_params=pltpu.CompilerParams(
             collective_id=0, has_side_effects=True, vmem_limit_bytes=VMEM_BYTES - kept - 4096

time: 36.8 us -> 36.7 us (level)
  no operation moved by 1% of the time
where the time goes in v5:
time: 36.7 us; the launch traced here: 36.5 us
  Pallas kernels  35.7 us (97%)
  between operations  0.8 us (2%)
    pallas_call x1, Pallas kernels, on_device(): pl.pallas_call(functools.partial(kernel, frames, fsdp, heads_axis, width,...  34.2 us
    pallas_call x1, Pallas kernels, on_device(): pl.pallas_call(write_out, out_shape=tuple((jax.ShapeDtypeStruct(out.shape...  1.54 us

profile of v5, /device:TPU:0, one launch (start us, length us, event | category | flops | bytes accessed | tf_op | source)
XLA Modules:
  0.0 36.5 jit_solution(17540624570534396430)
XLA Ops:
  0.6 34.2 %attention.1 = (bf16[256,1280]{1,0:T(8,128)(2,1)S(1)}, bf16[256,1280]{1,0:T(8,128)(2,1)S(1)}, bf16[256,1280]{1,0:T(8,128)(2,1)S(1)}, bf16[256,1280]{1,0:T(8,128)...) custom-call(bf16[256,1280]{1,0:T(8,128)(2,1)} %q_hbm.1, bf16[256,1280]{1,0:T(8,128)(2,1)} %k_hbm.1, ...), custom_call_target="tpu_custom_call" | custom-call | tf_op jit(solution)/shard_map/attention/pallas_call | solution.py:701
  34.8 1.5 %write_out.1 = (bf16[256,1280]{1,0:T(8,128)(2,1)}, bf16[256,1280]{1,0:T(8,128)(2,1)}, bf16[256,1280]{1,0:T(8,128)(2,1)}, bf16[256,1280]{1,0:T(8,128)(2,1)}, f32[1,5120]{1,0:T(1,128)}, /*index=5*/f32[1,5120]{1,0:T(1,128)}) custom-call(bf16[256,1280]{1,0:T(8,128)(2,1)S(1)} %get-tuple-element.18.refs_0_, bf16[256,1280]{1,0:T(8,128)(2,1)S(1)} %get-tuple-element.19.refs_1_, ...), custom_call_target="tpu_custom_call" | custom-call | tf_op jit(solution)/shard_map/write_out/pallas_call | solution.py:763

commit v6 on v5

--- a/solution.py
+++ b/solution.py
@@ -455,20 +455,27 @@
         sums1[high] = sums[...] + addend
         repeat(1, n1, lambda d: s1_copy(d, sums1.at[high]).start())
 
-    def end_copy(d, part):
-        p = lax.rem((frame * fsdp + fs) * heads_axis + lax.axis_index("head") + d, devices)
+    def end_copy(target, part):
         return pltpu.make_async_remote_copy(
             src_ref=part,
             dst_ref=part,
             send_sem=end_send.at[0],
             recv_sem=end_recv.at[0],
-            device_id={
-                "frame": p // (fsdp * heads_axis),
-                "fsdp": lax.rem(p // heads_axis, fsdp),
-                "head": lax.rem(p, heads_axis),
-            },
+            device_id=target,
             device_id_type=MESH,
         )
+
+    def send_ends(part):
+        rows = [lax.rem(frame + a, frames) for a in range(frames)]
+        heads = [lax.rem(lax.axis_index("head") + c, heads_axis) for c in range(heads_axis)]
+
+        def column(b, skip):
+            at = lax.rem(fs + b, fsdp)
+            for a, c in [(a, c) for a in range(frames) for c in range(heads_axis)][skip:]:
+                end_copy({"frame": rows[a], "fsdp": at, "head": heads[c]}, part).start()
+
+        repeat(1, fsdp, lambda b: column(b, 0))
+        column(0, 1)
 
     last = pl.ds((kept - 1) * DH, 2 * DH)
 
@@ -534,12 +541,12 @@
                 repeat(0, kept, step)
                 traded(1, other)
                 near_second(nb, batches[1])
+                end = me2 * slots + high
+                ends[end] = sums[:, last]
+                send_ends(ends.at[end])
                 row_copy(other).wait_recv()
                 rows = as_rows(inner_q[...], inner_k[...])
                 stats_go(1, jnp.where(row == 0, rows + row_in[0:1], rows))
-                end = me2 * slots + high
-                ends[end] = sums[:, last]
-                repeat(1, devices, lambda d: end_copy(d, ends.at[end]).start())
             else:
 
                 def step(h):
@@ -620,8 +627,8 @@
         gain_q_out[:, p * width : (p + 1) * width] = sums2[p, 0:1, :]
         gain_k_out[:, p * width : (p + 1) * width] = sums2[p, 1:2, :]
     if lent:
-        only(helps, end_copy(1, ends.at[pl.ds(0, n2 * slots)]).wait_recv)
-        only(helped, end_copy(1, ends.at[pl.ds(0, n2 * slots - 1)]).wait_recv)
+        only(helps, end_copy(peer2(1), ends.at[pl.ds(0, n2 * slots)]).wait_recv)
+        only(helped, end_copy(peer2(1), ends.at[pl.ds(0, n2 * slots - 1)]).wait_recv)
         for p in range(n2):
             late = jnp.sum(ends[pl.ds(p * slots, slots)], axis=0)
             cols = pl.ds(p * width + (kept - 1) * DH, 2 * DH)
@@ -643,7 +650,7 @@
     stats_copy(0, 1, stats.at[:, pl.ds(0, n2 - 1)]).wait_send()
     if lent:
         only(helped, s1_copy(1, sums1.at[pl.ds(0, n1 - 1)]).wait_send)
-        only(helped, end_copy(1, ends.at[pl.ds(0, devices - 1)]).wait_send)
+        only(helped, end_copy(peer2(1), ends.at[pl.ds(0, devices - 1)]).wait_send)
         only(helps, lambda: sum_copy(2).wait_send())
     else:
         s1_copy(1, sums1.at[pl.ds(0, n1 - 1)]).wait_send()

time: 36.7 us -> 36.6 us (level)
  no operation moved by 1% of the time
where the time goes in v6:
time: 36.6 us; the launch traced here: 36.4 us
  Pallas kernels  35.6 us (97%)
  between operations  0.8 us (2%)
    pallas_call x1, Pallas kernels, on_device(): pl.pallas_call(functools.partial(kernel, frames, fsdp, heads_axis, width,...  34.1 us
    pallas_call x1, Pallas kernels, on_device(): pl.pallas_call(write_out, out_shape=tuple((jax.ShapeDtypeStruct(out.shape...  1.54 us

profile of v6, /device:TPU:0, one launch (start us, length us, event | category | flops | bytes accessed | tf_op | source)
XLA Modules:
  0.0 36.4 jit_solution(12649025100593922391)
XLA Ops:
  0.6 34.1 %attention.1 = (bf16[256,1280]{1,0:T(8,128)(2,1)S(1)}, bf16[256,1280]{1,0:T(8,128)(2,1)S(1)}, bf16[256,1280]{1,0:T(8,128)(2,1)S(1)}, bf16[256,1280]{1,0:T(8,128)...) custom-call(bf16[256,1280]{1,0:T(8,128)(2,1)} %q_hbm.1, bf16[256,1280]{1,0:T(8,128)(2,1)} %k_hbm.1, ...), custom_call_target="tpu_custom_call" | custom-call | tf_op jit(solution)/shard_map/attention/pallas_call | solution.py:708
  34.7 1.5 %write_out.1 = (bf16[256,1280]{1,0:T(8,128)(2,1)}, bf16[256,1280]{1,0:T(8,128)(2,1)}, bf16[256,1280]{1,0:T(8,128)(2,1)}, bf16[256,1280]{1,0:T(8,128)(2,1)}, f32[1,5120]{1,0:T(1,128)}, /*index=5*/f32[1,5120]{1,0:T(1,128)}) custom-call(bf16[256,1280]{1,0:T(8,128)(2,1)S(1)} %get-tuple-element.18.refs_0_, bf16[256,1280]{1,0:T(8,128)(2,1)S(1)} %get-tuple-element.19.refs_1_, ...), custom_call_target="tpu_custom_call" | custom-call | tf_op jit(solution)/shard_map/write_out/pallas_call | solution.py:770
